TPU v7x, 128 devices: a whole 4x4x4 slice. The times are simulated.
128 devices in a mesh: gx: 8 (over z_hi, x), gy: 4 (over z_lo, core), gz: 4 (over y).
Axes of the slice: x: 4, y: 4, z: 4 (z_hi: 2, z_lo: 2; z = z_hi * 2 + z_lo), core: 2. Of those that a mesh axis runs over, the one named last changes fastest.
Arguments:
- calcium: float32 [8, 256, 128, 512], P(None, 'gx', 'gz', 'gy'), may hold values from 0.1 to 3
- activation: float32 [8, 256, 128, 512], P(None, 'gx', 'gz', 'gy'), may hold values from 0 to 1
- element_first: int32 [256], replicated, may hold values from 0 to 63, as said below
- offset_first: float32 [256], replicated, may hold values from 0.1 to 0.9
- element_second: int32 [512], replicated, may hold values from 0 to 127, as said below
- offset_second: float32 [512], replicated, may hold values from 0.1 to 0.9
- element_third: int32 [128], replicated, may hold values from 0 to 31, as said below
- offset_third: float32 [128], replicated, may hold values from 0.1 to 0.9
- troponin: float32 [64, 32, 128], P('gx', ('gy', 'gz')), may hold values from 0 to 1
- tension: float32 [64, 32, 128], P('gx', ('gy', 'gz')), may hold values from 0 to 2
- unbind_rate: float32 [64, 32, 128], P('gx', ('gy', 'gz')), may hold values from 0.2 to 2
- relax_rate: float32 [64, 32, 128], P('gx', ('gy', 'gz')), may hold values from 0.5 to 4
Outputs:
- bound_fraction: float32 [64, 32, 128], P('gx', ('gy', 'gz'))
- active_tension: float32 [64, 32, 128], P('gx', ('gy', 'gz'))
Inputs may be any that keep to these rules, and one draw needn't show every extreme that they name: `element_first`: never falling; the cells of each aligned block of 32 cells belong to that block's own 8 elements, each element holding at least one cell. `element_second`: never falling; the cells of each aligned block of 128 cells belong to that block's own 32 elements, each element holding at least one cell. `element_third`: never falling; the cells of each aligned block of 8 cells belong to that block's own 2 elements, each element holding at least one cell.
All inputs are finite; a program needn't handle non-finite values.
Results may differ from a plain program's by a relative error of at most 0.00005.
Values sent between devices are 32-bit elements.
A program may use at most 64 MiB of HBM per device.

v0:
```python
import jax
import jax.numpy as jnp
from jax import lax
from jax.sharding import PartitionSpec as P

highest = lax.Precision.HIGHEST
step_size = 0.2
bind_rate = 2.0
peak_tension = 2.0
half_square = 0.25


def shifted(x, axis, by):
    length = lax.axis_size(axis)
    pairs = [(i, i + by) for i in range(length) if 0 <= i + by < length]
    return lax.ppermute(x, axis, pairs)


def axis_weights(element, offset, first_node, count, first_cell, cells):
    node_ids = first_node + jnp.arange(count, dtype=jnp.int32)
    inside = element[None, :] == node_ids[:, None]
    following = element[None, :] + 1 == node_ids[:, None]
    raw_weights = jnp.where(inside, 1.0 - offset[None, :], 0.0) + jnp.where(
        following, offset[None, :], 0.0
    )
    scaled = raw_weights / jnp.sum(raw_weights, axis=1, keepdims=True)
    return lax.dynamic_slice_in_dim(scaled, first_cell, cells, 1)


def restrict_block(field, weight_row, weight_depth, weight_col):
    section = jnp.einsum("ai,sizy->sazy", weight_row, field, precision=highest)
    section = jnp.einsum("bz,sazy->saby", weight_depth, section, precision=highest)
    return jnp.einsum("cy,saby->sabc", weight_col, section, precision=highest)


def last_layer(partial_value, dim):
    extent = partial_value.shape[dim]
    return lax.slice_in_dim(partial_value, extent - 1, extent, axis=dim)


def merge_edge(partial_value, incoming, dim):
    extent = partial_value.shape[dim]
    leading = lax.slice_in_dim(partial_value, 0, 1, axis=dim) + incoming
    middle = lax.slice_in_dim(partial_value, 1, extent - 1, axis=dim)
    return lax.concatenate([leading, middle], dim)


def fold_rows(partial_value):
    incoming = shifted(last_layer(partial_value, 2), "gx", 1)
    return merge_edge(partial_value, incoming, 2)


def tension_steps(drivers, troponin, tension, unbind_rate, relax_rate):
    bound = troponin
    active = tension
    for substep in range(drivers.shape[1]):
        calcium_now = drivers[0, substep]
        squared = calcium_now * calcium_now
        binding = squared / (squared + half_square)
        bound = bound + step_size * (bind_rate * binding * (1.0 - bound) - unbind_rate * bound)
        active = active + step_size * relax_rate * (
            peak_tension * drivers[1, substep] * bound - active
        )
    return (bound, active)


def per_device(
    calcium,
    activation,
    element_first,
    offset_first,
    element_second,
    offset_second,
    element_third,
    offset_third,
    troponin,
    tension,
    unbind_rate,
    relax_rate,
):
    sub_count, fine_rows, fine_depth, fine_cols = calcium.shape
    nodes_x, nodes_block, nodes_all_y = troponin.shape
    groups = lax.axis_size("gz")
    row_index = lax.axis_index("gx")
    weight_row = axis_weights(
        element_first,
        offset_first,
        row_index * nodes_x,
        nodes_x + 1,
        row_index * fine_rows,
        fine_rows,
    )
    slab_index = lax.axis_index("gz")
    col_index = lax.axis_index("gy")
    slab_nodes = nodes_block * groups
    nodes_y = nodes_all_y // lax.axis_size("gy")
    weight_depth = axis_weights(
        element_third,
        offset_third,
        slab_index * slab_nodes,
        slab_nodes + 1,
        slab_index * fine_depth,
        fine_depth,
    )
    weight_col = axis_weights(
        element_second,
        offset_second,
        col_index * nodes_y,
        nodes_y + 1,
        col_index * fine_cols,
        fine_cols,
    )
    partial_value = jnp.stack(
        [
            restrict_block(field, weight_row, weight_depth, weight_col)
            for field in (calcium, activation)
        ]
    )
    partial_value = fold_rows(partial_value)
    incoming = shifted(last_layer(partial_value, 3), "gz", 1)
    partial_value = merge_edge(partial_value, incoming, 3)
    incoming = shifted(last_layer(partial_value, 4), "gy", 1)
    partial_value = merge_edge(partial_value, incoming, 4)
    shaped = partial_value.reshape(2, 1, sub_count, nodes_x, groups, nodes_block, nodes_y)
    regrouped = lax.all_to_all(
        lax.all_to_all(shaped, "gz", split_axis=4, concat_axis=1, tiled=True),
        "gy",
        split_axis=1,
        concat_axis=6,
        tiled=True,
    )
    drivers = regrouped.reshape(2, sub_count, nodes_x, nodes_block, nodes_all_y)
    return tension_steps(drivers, troponin, tension, unbind_rate, relax_rate)


def solution(mesh):
    return jax.shard_map(
        per_device,
        mesh=mesh,
        in_specs=(
            P(None, "gx", "gz", "gy"),
            P(None, "gx", "gz", "gy"),
            P(),
            P(),
            P(),
            P(),
            P(),
            P(),
            P("gx", ("gy", "gz"), None),
            P("gx", ("gy", "gz"), None),
            P("gx", ("gy", "gz"), None),
            P("gx", ("gy", "gz"), None),
        ),
        out_specs=(P("gx", ("gy", "gz"), None), P("gx", ("gy", "gz"), None)),
        check_vma=False,
    )
```

profile of v0, /device:TPU:64, one launch (start us, length us, event | category | flops | bytes accessed | tf_op | source)
XLA Modules:
  0.0 76.5 jit_solution(3353908300867582701)
XLA Ops:
  0.6 0.7 broadcast_add_fusion.1
  1.3 0.7 broadcast_subtract_fusion.1
  2.0 0.7 broadcast_add_fusion.2
  2.7 0.7 broadcast_subtract_fusion.2
  3.3 0.7 broadcast_add_fusion
  4.0 0.7 broadcast_subtract_fusion
  4.7 0.9 %fusion.127 = (f32[9]{0:T(128)S(1)}, f32[9,256]{1,0:T(8,128)S(1)}) fusion(f32[256]{0:T(256)} %param.15, s32[256]{0:T(256)S(1)} %broadcast_add_fusion.1, f32[256]{0:T(256)S(1)} %broadcast_subtract_fusion.1, s32[9]{0:T(128)S(1)} %iota_add_fusion.2, s32[256]{0:T(256)} %param.14), kind=kLoop, calls=%fused_computation.170 | loop fusion | flops 13815 | bytes 13384 | tf_op jit(solution)/shard_map/reduce_sum | solution.py:26
  5.6 7.9 %fusion.4 = f32[8,9,32,128]{3,1,2,0:T(8,128)} fusion(f32[8,32,32,128]{3,2,1,0:T(8,128)} %param.12, f32[9,256]{1,0:T(8,128)S(1)} %get-tuple-element.9, s32[]{:T(128)S(6)} %select_n.32, f32[9]{0:T(128)S(1)} %get-tuple-element.8), kind=kOutput, calls=%fused_computation.4 | convolution fusion | flops 113246496 | bytes 5382660 | tf_op jit(solution)/shard_map/ai,sizy->sazy/dot_general | solution.py:31
  13.5 4.4 %fusion.7 = f32[8,9,32,128]{3,1,2,0:T(8,128)S(1)} fusion(f32[8,32,32,128]{3,2,1,0:T(8,128)S(1)} %copy-done, f32[9,256]{1,0:T(8,128)S(1)} %get-tuple-element.9, s32[]{:T(128)S(6)} %select_n.32, f32[9]{0:T(128)S(1)} %get-tuple-element.8), kind=kOutput, calls=%fused_computation.5 | convolution fusion | flops 113246496 | bytes 5382660 | tf_op jit(solution)/shard_map/ai,sizy->sazy/dot_general | solution.py:31
  18.2 2.6 %convolution_bitcast_fusion.3 = f32[8,9,9,128]{3,2,1,0:T(8,128)S(1)} fusion(f32[8,9,32,128]{3,1,2,0:T(8,128)} %fusion.4, f32[9,128]{1,0:T(8,128)S(1)} %get-tuple-element.11, s32[]{:T(128)S(6)} %select_n.35, f32[9]{0:T(128)S(1)} %get-tuple-element.10), kind=kOutput, calls=%fused_computation.9 | convolution fusion | flops 31850784 | bytes 1516072 | tf_op jit(solution)/shard_map/bz,sazy->saby/dot_general | solution.py:32
  20.8 1.1 %convolution_bitcast_fusion.1 = f32[8,9,9,128]{3,2,1,0:T(8,128)S(1)} fusion(f32[8,9,32,128]{3,1,2,0:T(8,128)S(1)} %fusion.7, f32[9,128]{1,0:T(8,128)S(1)} %get-tuple-element.11, s32[]{:T(128)S(6)} %select_n.35, f32[9]{0:T(128)S(1)} %get-tuple-element.10), kind=kOutput, calls=%fused_computation.7 | convolution fusion | flops 31850784 | bytes 1516072 | tf_op jit(solution)/shard_map/bz,sazy->saby/dot_general | solution.py:32
  22.1 0.9 %convolution_bitcast_fusion.2 = f32[1,8,9,9,33]{4,3,2,1,0:T(8,128)S(1)} fusion(f32[8,9,9,128]{3,2,1,0:T(8,128)S(1)} %convolution_bitcast_fusion.3, f32[33,512]{1,0:T(8,128)S(1)} %get-tuple-element.7, s32[]{:T(128)S(6)} %select_n.38, f32[33]{0:T(128)S(1)} %get-tuple-element.6), kind=kOutput, calls=%fused_computation.8 | convolution fusion | flops 32850048 | bytes 696356 | tf_op jit(solution)/shard_map/cy,saby->sabc/dot_general | solution.py:33
  22.9 0.7 convolution_bitcast_fusion
  23.7 3.4 %collective-permute-start = (f32[2,8,1,9,33]{4,3,2,1,0:T(8,128)S(1)}, f32[2,8,1,9,33]{4,3,2,1,0:T(8,128)S(1)}, u32[]{:S(2)}, u32[]{:S(2)}) collective-permute-start(f32[2,8,1,9,33]{4,3,2,1,0:T(8,128)S(1)} %pad_maximum_fusion), channel_id=1, source_target_pairs={{0,16},{16,32},{32,48},{48,64},{64,80},{80,96},{96,112},{1,17},{17... | collective-permute-start | bytes 57032 | tf_op jit(solution)/shard_map/ppermute | solution.py:16
  27.1 7.3 %collective-permute-done = f32[2,8,1,9,33]{4,3,2,1,0:T(8,128)S(1)} collective-permute-done((f32[2,8,1,9,33]{4,3,2,1,0:T(8,128)S(1)}, f32[2,8,1,9,33]{4,3,2,1,0:T(8,128)S(1)}, u32[]{:S(2)}, u32[]{:S(2)}) %collective-permute-start) | collective-permute-done | bytes 19040 | tf_op jit(solution)/shard_map/ppermute | solution.py:16
  34.6 3.5 %collective-permute-start.1 = (f32[2,8,8,1,33]{4,3,2,1,0:T(1,128)S(1)}, f32[2,8,8,1,33]{4,3,2,1,0:T(1,128)S(1)}, u32[]{:S(2)}, u32[]{:S(2)}) collective-permute-start(f32[2,8,8,1,33]{4,3,2,1,0:T(1,128)S(1)} %slice.101), channel_id=1, source_target_pairs={{0,1},{1,2},{2,3},{4,5},{5,6},{6,7},{8,9},{9,10},{10,11},{12,13},{... | collective-permute-start | bytes 50696 | tf_op jit(solution)/shard_map/ppermute | solution.py:16
  38.1 1.8 %collective-permute-done.1 = f32[2,8,8,1,33]{4,3,2,1,0:T(1,128)S(1)} collective-permute-done((f32[2,8,8,1,33]{4,3,2,1,0:T(1,128)S(1)}, f32[2,8,8,1,33]{4,3,2,1,0:T(1,128)S(1)}, u32[]{:S(2)}, u32[]{:S(2)}) %collective-permute-start.1) | collective-permute-done | bytes 16928 | tf_op jit(solution)/shard_map/ppermute | solution.py:16
  40.4 1.3 %collective-permute-start.2 = (f32[2,8,8,8,1]{4,3,2,1,0:T(8,128)S(1)}, f32[2,8,8,8,1]{4,3,2,1,0:T(8,128)S(1)}, u32[]{:S(2)}, u32[]{:S(2)}) collective-permute-start(f32[2,8,8,8,1]{4,3,2,1,0:T(8,128)S(1)} %fusion.13), channel_id=1, source_target_pairs={{0,4},{4,8},{8,12},{1,5},{5,9},{9,13},{2,6},{6,10},{10,14},{3,7},{... | collective-permute-start | bytes 12296 | tf_op jit(solution)/shard_map/ppermute | solution.py:16
  41.7 1.5 %collective-permute-done.2 = f32[2,8,8,8,1]{4,3,2,1,0:T(8,128)S(1)} collective-permute-done((f32[2,8,8,8,1]{4,3,2,1,0:T(8,128)S(1)}, f32[2,8,8,8,1]{4,3,2,1,0:T(8,128)S(1)}, u32[]{:S(2)}, u32[]{:S(2)}) %collective-permute-start.2) | collective-permute-done | bytes 4128 | tf_op jit(solution)/shard_map/ppermute | solution.py:16
  44.3 11.0 %all_to_all.33 = f32[4,1,8192]{2,1,0:T(1,128)S(1)} all-to-all(f32[4,1,8192]{2,1,0:T(1,128)S(1)} %reshape.73), channel_id=1, replica_groups=mesh['gx'=8,'gy'=4,'gz'=4] {'gz'}, dimensions={0} | all-to-all | bytes 262144 | tf_op jit(solution)/shard_map/all_to_all | solution.py:126
  55.8 1.0 %reduce = f32[4,8192]{1,0:T(4,128)S(1)} reduce(f32[4,1,8192]{2,1,0:T(1,128)S(1)} %all_to_all.33, f32[]{:T(128)} %broadcast.223), dimensions={1}, to_apply=%all_to_all.24.reduce_sub_computation | reduce | bytes 262148 | tf_op jit(solution)/shard_map/all_to_all | solution.py:126
  57.9 15.1 %all_to_all.34 = f32[4,1,8192]{2,1,0:T(1,128)S(1)} all-to-all(f32[4,1,8192]{2,1,0:T(1,128)S(1)} %reshape.75), channel_id=1, replica_groups=mesh['gx'=8,'gy'=4,'gz'=4] {'gy'}, dimensions={0} | all-to-all | bytes 262144 | tf_op jit(solution)/shard_map/all_to_all | solution.py:125
  73.0 1.0 %reduce.1 = f32[4,8192]{1,0:T(4,128)S(1)} reduce(f32[4,1,8192]{2,1,0:T(1,128)S(1)} %all_to_all.34, f32[]{:T(128)} %broadcast.223), dimensions={1}, to_apply=%all_to_all.28.reduce_sub_computation | reduce | bytes 262148 | tf_op jit(solution)/shard_map/all_to_all | solution.py:125
  75.2 0.6 copy.38
  (44 shorter events, 5.5 us)
Async XLA Ops:
  5.6 7.9 %copy-start = (f32[8,32,32,128]{3,2,1,0:T(8,128)S(1)}, f32[8,32,32,128]{3,2,1,0:T(8,128)}, u32[]{:S(2)}) copy-start(f32[8,32,32,128]{3,2,1,0:T(8,128)} %param.13) | copy-start | bytes 12582916
  13.5 4.4 %copy-start.7 = (f32[128]{0:T(128)S(1)}, f32[128]{0:T(128)}, u32[]{:S(2)}) copy-start(f32[128]{0:T(128)} %param.19) | copy-start | bytes 1540
  13.5 4.4 %copy-start.8 = (s32[128]{0:T(128)S(1)}, s32[128]{0:T(128)}, u32[]{:S(2)}) copy-start(s32[128]{0:T(128)} %param.18) | copy-start | bytes 1540
  17.9 3.9 %copy-start.5 = (f32[512]{0:T(512)S(1)}, f32[512]{0:T(512)}, u32[]{:S(2)}) copy-start(f32[512]{0:T(512)} %param.17) | copy-start | bytes 6148
  17.9 3.9 %copy-start.6 = (s32[512]{0:T(512)S(1)}, s32[512]{0:T(512)}, u32[]{:S(2)}) copy-start(s32[512]{0:T(512)} %param.16) | copy-start | bytes 6148
  23.7 10.7 %collective-permute-start = (f32[2,8,1,9,33]{4,3,2,1,0:T(8,128)S(1)}, f32[2,8,1,9,33]{4,3,2,1,0:T(8,128)S(1)}, u32[]{:S(2)}, u32[]{:S(2)}) collective-permute-start(f32[2,8,1,9,33]{4,3,2,1,0:T(8,128)S(1)} %pad_maximum_fusion), channel_id=1, source_target_pairs={{0,16},{16,32},{32,48},{48,64},{64,80},{80,96},{96,112},{1,17},{17... | collective-permute-start | bytes 57032 | tf_op jit(solution)/shard_map/ppermute | solution.py:16
  34.6 5.4 %collective-permute-start.1 = (f32[2,8,8,1,33]{4,3,2,1,0:T(1,128)S(1)}, f32[2,8,8,1,33]{4,3,2,1,0:T(1,128)S(1)}, u32[]{:S(2)}, u32[]{:S(2)}) collective-permute-start(f32[2,8,8,1,33]{4,3,2,1,0:T(1,128)S(1)} %slice.101), channel_id=1, source_target_pairs={{0,1},{1,2},{2,3},{4,5},{5,6},{6,7},{8,9},{9,10},{10,11},{12,13},{... | collective-permute-start | bytes 50696 | tf_op jit(solution)/shard_map/ppermute | solution.py:16
  40.4 2.8 %collective-permute-start.2 = (f32[2,8,8,8,1]{4,3,2,1,0:T(8,128)S(1)}, f32[2,8,8,8,1]{4,3,2,1,0:T(8,128)S(1)}, u32[]{:S(2)}, u32[]{:S(2)}) collective-permute-start(f32[2,8,8,8,1]{4,3,2,1,0:T(8,128)S(1)} %fusion.13), channel_id=1, source_target_pairs={{0,4},{4,8},{8,12},{1,5},{5,9},{9,13},{2,6},{6,10},{10,14},{3,7},{... | collective-permute-start | bytes 12296 | tf_op jit(solution)/shard_map/ppermute | solution.py:16
  57.9 17.3 %copy-start.1 = (f32[8,2,128]{2,1,0:T(2,128)S(1)}, f32[8,2,128]{2,1,0:T(2,128)}, u32[]{:S(2)}) copy-start(f32[8,2,128]{2,1,0:T(2,128)} %param.21) | copy-start | bytes 24580
  57.9 17.3 %copy-start.2 = (f32[8,2,128]{2,1,0:T(2,128)S(1)}, f32[8,2,128]{2,1,0:T(2,128)}, u32[]{:S(2)}) copy-start(f32[8,2,128]{2,1,0:T(2,128)} %param.23) | copy-start | bytes 24580
  57.9 17.3 %copy-start.3 = (f32[8,2,128]{2,1,0:T(2,128)S(1)}, f32[8,2,128]{2,1,0:T(2,128)}, u32[]{:S(2)}) copy-start(f32[8,2,128]{2,1,0:T(2,128)} %param.22) | copy-start | bytes 24580
  57.9 17.3 %copy-start.4 = (f32[8,2,128]{2,1,0:T(2,128)S(1)}, f32[8,2,128]{2,1,0:T(2,128)}, u32[]{:S(2)}) copy-start(f32[8,2,128]{2,1,0:T(2,128)} %param.20) | copy-start | bytes 24580
where the time goes:
time: 76.9 us; the launch traced here: 76.5 us
  blocking collectives  26.1 us (34%)
  matrix products  17.6 us (23%)
  waiting for transfers between devices  10.7 us (14%)
  other arithmetic  8.23 us (11%)
  starting transfers between devices  8.2 us (11%)
  local copies, waits for them, and re-layouts  4.72 us (6%)
  between operations  0.96 us (1%)
    all_to_all x1, blocking collectives, per_device(): lax.all_to_all(lax.all_to_all(shaped, 'gz', split_axis=4, concat_axis=1,...  15.1 us
    dot_general x2, matrix products, restrict_block(): section = jnp.einsum('ai,sizy->sazy', weight_row, field, precision=highest)  12.3 us
    all_to_all x1, blocking collectives, per_device(): lax.all_to_all(shaped, 'gz', split_axis=4, concat_axis=1, tiled=True)  11 us
    ppermute x3, waiting for transfers between devices, shifted(): return lax.ppermute(x, axis, pairs)  10.7 us
    ppermute x3, starting transfers between devices, shifted(): return lax.ppermute(x, axis, pairs)  8.2 us
    dot_general x2, matrix products, restrict_block(): jnp.einsum('bz,sazy->saby', weight_depth, section, precision=highest)  3.69 us
    unnamed x25, local copies, waits for them, and re-layouts  3.29 us
    add x3, other arithmetic, axis_weights(): following = element[None, :] + 1 == node_ids[:, None]  2.02 us
  transfers between devices with their start and end apart: 3, of which 3 were waited for; matrix products, arithmetic and copies ran while one was open for 0% of the time, Pallas kernels for 0%

commit v1 on v0

v1 whole, which is shorter than its diff:
```python
import functools

import jax
import jax.numpy as jnp
from jax import lax
from jax.experimental import pallas as pl
from jax.experimental.pallas import tpu as pltpu
from jax.sharding import PartitionSpec as P

step_size = 0.2
bind_rate = 2.0
peak_tension = 2.0
half_square = 0.25
MESH = pl.DeviceIdType.MESH
f32 = jnp.float32
bf16 = jnp.bfloat16

SLABS = 4
BLOCKS = 4
ROWS = 32
CHUNKS = 4
MAIN = CHUNKS * 16 + 16
EDGE = CHUNKS * 8 + 8


def raw_weights(element, offset, node):
    return jnp.where(element == node, 1.0 - offset, 0.0) + jnp.where(
        element + 1 == node, offset, 0.0
    )


def split(x):
    high = x.astype(bf16)
    low = (x - high.astype(f32)).astype(bf16)
    return high, low


def dot(a, b):
    return jnp.dot(a, b, preferred_element_type=f32)


def iota(shape, dim):
    return lax.broadcasted_iota(jnp.int32, shape, dim)


def spread(element, offset, pick):
    cells = element.shape[1]
    first = offset.astype(bf16).astype(f32)
    second = (offset - first).astype(bf16).astype(f32)
    third = offset - first - second
    row = iota((16, cells), 0)
    stack = jnp.where(
        row == 0,
        element.astype(f32),
        jnp.where(row == 1, first, jnp.where(row == 2, second, jnp.where(row == 3, third, 0.0))),
    )
    out = dot(stack.astype(bf16), pick)
    return out[0:1], out[1:2] + out[2:3] + out[3:4]


def kernel(
    cal, act, ef, of, es, os_, et, ot, trop, tens, unb, rel,
    out_bound, out_active,
    x_buf, ef_v, of_v, es_v, os_v, et_v, ot_v, trop_v, tens_v, unb_v, rel_v,
    w1, w2h, w2l,
    s_main, s_x, s_edge, s_corner,
    r_main, r_x, r_edge, r_corner,
    sem_x, sem_small,
    ss_main, ss_x, ss_edge, ss_corner,
    rs_main, rs_x, rs_edge, rs_corner,
):
    gx, gy, gz = lax.axis_index("gx"), lax.axis_index("gy"), lax.axis_index("gz")
    last_x = lax.axis_size("gx") - 1
    blocks = [lax.rem(gz + 1 + j, BLOCKS) for j in range(BLOCKS)]

    smalls = [
        pltpu.make_async_copy(src, dst, sem_small.at[n])
        for n, (src, dst) in enumerate(
            [(ef, ef_v), (of, of_v), (et, et_v), (ot, ot_v), (es, es_v), (os_, os_v),
             (trop, trop_v), (tens, tens_v), (unb, unb_v), (rel, rel_v)]
        )
    ]
    for copy in smalls:
        copy.start()
    loads = {}
    for j in range(BLOCKS):
        first_cell = pl.multiple_of(blocks[j] * 8, 8)
        for u in range(CHUNKS):
            src = (cal, act)[u // 2].at[pl.ds(4 * (u % 2), 4), :, pl.ds(first_cell, 8), :]
            loads[j, u] = pltpu.make_async_copy(src, x_buf.at[j, u], sem_x.at[j, u])
            loads[j, u].start()

    from_below = jnp.logical_and(gz == 0, gy > 0)
    has_edge = jnp.logical_or(from_below, gz == gy + 1)
    has_x = gx > 0
    sends_x = gx < last_x
    sends_edge = gz < SLABS - 1

    def main_self(c):
        return jnp.logical_and(gy == gz, gy == c)

    def below_self(c):
        return jnp.logical_and(jnp.logical_and(gy == 1, gz == 0), gy == c)

    barrier = pltpu.get_barrier_semaphore()

    def ready(x, y, z):
        pl.semaphore_signal(
            barrier, inc=1, device_id={"gx": x, "gy": y, "gz": z}, device_id_type=MESH
        )

    for c in range(4):
        @pl.when(jnp.logical_not(main_self(c)))
        def _():
            ready(gx, c, gy)

        @pl.when(jnp.logical_and(from_below, jnp.logical_not(below_self(c))))
        def _():
            ready(gx, c, gy - 1)

        @pl.when(has_x)
        def _():
            ready(gx - 1, c, gy)

        @pl.when(jnp.logical_and(has_x, from_below))
        def _():
            ready(gx - 1, c, gy - 1)

    edge_self = jnp.logical_and(gz == 0, gy == 1)
    expected = (
        jnp.where(gy == gz, 3, 4)
        + jnp.where(sends_x, 4, 0)
        + jnp.where(jnp.logical_and(sends_edge, jnp.logical_not(edge_self)), 1, 0)
        + jnp.where(jnp.logical_and(sends_edge, sends_x), 1, 0)
    )

    @pl.when(jnp.logical_not(has_x))
    def _():
        r_x[...] = jnp.zeros_like(r_x)

    @pl.when(jnp.logical_not(has_edge))
    def _():
        r_edge[...] = jnp.zeros_like(r_edge)

    @pl.when(jnp.logical_not(jnp.logical_and(has_x, has_edge)))
    def _():
        r_corner[...] = jnp.zeros_like(r_corner)

    row = iota((ROWS, 1), 0)
    a_of = jnp.where(row < 24, lax.rem(row, 8), 8)
    b_of = jnp.where(row < 24, row // 8, row - 24)
    valid = row < 27
    pick_first = jnp.where(iota((256, 256), 0) == 32 * gx + iota((256, 256), 1) // 8, 1.0, 0.0).astype(bf16)
    pick_cell = iota((128, 256), 0) - lax.rem(iota((128, 256), 1), 8)
    for n in range(4):
        smalls[n].wait()
    e_first = jnp.concatenate([ef_v[0:1, :], ef_v[1:2, :]], axis=1)
    o_first = jnp.concatenate([of_v[0:1, :], of_v[1:2, :]], axis=1)
    node_first = 8 * gx + a_of
    sum_first = jnp.sum(raw_weights(e_first, o_first, node_first), axis=1, keepdims=True)
    ex, ox = spread(e_first, o_first, pick_first)
    wide_first = raw_weights(ex, ox, node_first.astype(f32))
    e_third, o_third = et_v[...], ot_v[...]
    for j in range(BLOCKS):
        node_third = 8 * gz + 2 * blocks[j] + b_of
        sum_third = jnp.sum(raw_weights(e_third, o_third, node_third), axis=1, keepdims=True)
        pick = jnp.where(pick_cell == 32 * gz + 8 * blocks[j], 1.0, 0.0).astype(bf16)
        ex, ox = spread(e_third, o_third, pick)
        scale = jnp.where(valid, 1.0 / jnp.where(valid, sum_first * sum_third, 1.0), 0.0)
        wide = wide_first * raw_weights(ex, ox, node_third.astype(f32)) * scale
        high, low = split(wide)
        w1[j, 0:ROWS] = high
        w1[j, ROWS:] = low

    smalls[4].wait()
    smalls[5].wait()
    node_row = iota((40, 1), 0)
    node_second = 32 * gy + node_row
    inside = jnp.logical_and(node_row < 33, node_second < 128)
    total = jnp.zeros((40, 1), f32)
    for n in range(4):
        total += jnp.sum(
            raw_weights(es_v[n : n + 1, :], os_v[n : n + 1, :], node_second), axis=1, keepdims=True
        )
    own = raw_weights(es_v[pl.ds(gy, 1), :], os_v[pl.ds(gy, 1), :], node_second)
    own = jnp.where(inside, own / jnp.where(inside, total, 1.0), 0.0)
    lane_w = iota((128, 128), 1)
    turned = jnp.transpose(jnp.concatenate([own[0:32]] * 4, axis=0))
    turned_edge = jnp.transpose(jnp.broadcast_to(own[32:33], (128, 128)))
    for k in range(4):
        group = lax.rem(gy + k, 4)
        edge_lane = 32 * lax.rem(gy + 1 + k, 4)
        wide = jnp.concatenate(
            [
                jnp.where(lane_w // 32 == group, turned, 0.0),
                jnp.where(lane_w == edge_lane, turned_edge, 0.0),
            ],
            axis=1,
        )
        high, low = split(wide)
        w2h[128 * k : 128 * (k + 1), :] = high
        w2l[128 * k : 128 * (k + 1), :] = low

    def remote(src, dst, send_sem, recv_sem, x, y, z):
        return pltpu.make_async_remote_copy(
            src_ref=src, dst_ref=dst, send_sem=send_sem, recv_sem=recv_sem,
            device_id={"gx": x, "gy": y, "gz": z}, device_id_type=MESH,
        )

    pending = []

    def send(when, copy):
        @pl.when(when)
        def _():
            copy.start()

        pending.append((when, copy))

    always = gx >= 0
    sub8 = iota((8, 128), 0)
    carry = None
    for j in range(BLOCKS):
        block = blocks[j]
        ys = []
        for u in range(CHUNKS):
            loads[j, u].wait()
            halves = []
            for pair in range(2):
                x = jnp.concatenate(
                    [x_buf[j, u, 2 * pair + n].reshape(256, 128) for n in range(2)], axis=1
                )
                high, low = split(x)
                both = dot(w1[j], high)
                halves.append(both[0:ROWS] + both[ROWS:] + dot(w1[j, 0:ROWS], low))
            ys.append(jnp.concatenate(halves, axis=1))
        y = jnp.concatenate(ys, axis=0)
        high, low = split(y)
        n = CHUNKS * ROWS
        both = dot(jnp.concatenate([high, low], axis=0), w2h[...])
        z = both[0:n] + both[n:] + dot(high, w2l[...])
        parts = [z[ROWS * u : ROWS * (u + 1), 0:128] for u in range(CHUNKS)]
        extra = z[0:ROWS, 128:256]
        for u in range(1, CHUNKS):
            extra += pltpu.roll(z[ROWS * u : ROWS * (u + 1), 128:256], u, axis=1)
        parts.append(extra)
        if carry is not None:
            use = block != 0
            merged = []
            for part, (rows8, corner) in zip(parts, carry):
                merged.append(
                    jnp.concatenate(
                        [
                            part[0:8] + jnp.where(use, rows8, 0.0),
                            part[8:24],
                            part[24:32] + jnp.where(jnp.logical_and(use, sub8 == 0), corner, 0.0),
                        ],
                        axis=0,
                    )
                )
            parts = merged
        carry = [(part[16:24], pltpu.roll(part[24:32], 6, axis=0)) for part in parts]
        for u in range(CHUNKS + 1):
            s_main[j, 16 * u : 16 * (u + 1), :] = parts[u][0:16]
            s_x[j, 2 * u : 2 * (u + 1), :] = parts[u][24:26]

        def store_edge(slot):
            for u in range(CHUNKS + 1):
                s_edge[slot, 8 * u : 8 * (u + 1), :] = parts[u][16:24]
                s_corner[slot, u : u + 1, :] = parts[u][26:27]

        up = jnp.logical_and(block == BLOCKS - 1, sends_edge)

        @pl.when(up)
        def _():
            store_edge(0)

        if j == BLOCKS - 1:
            @pl.when(sends_edge)
            def _():
                store_edge(1)

        if j == 0:
            pl.semaphore_wait(barrier, expected)

        send(
            sends_x,
            remote(s_x.at[j], r_x.at[gy], ss_x.at[j], rs_x.at[gy], gx + 1, gz, block),
        )
        main_copy = remote(
            s_main.at[j], r_main.at[gy], ss_main.at[j], rs_main.at[gy], gx, gz, block
        )
        if j < BLOCKS - 1:
            send(always, main_copy)
        else:
            send(gy != gz, main_copy)

            @pl.when(gy == gz)
            def _():
                r_main[pl.ds(gy, 1)] = s_main[pl.ds(j, 1)]

        @pl.when(jnp.logical_and(up, sends_x))
        def _():
            remote(
                s_corner.at[0], r_corner.at[gy], ss_corner.at[0], rs_corner.at[gy], gx + 1, gz + 1, 0
            ).start()

        @pl.when(jnp.logical_and(up, jnp.logical_not(edge_self)))
        def _():
            remote(
                s_edge.at[0], r_edge.at[gy], ss_edge.at[0], rs_edge.at[gy], gx, gz + 1, 0
            ).start()

        @pl.when(jnp.logical_and(up, edge_self))
        def _():
            r_edge[pl.ds(gy, 1)] = s_edge[0:1]

        if j == BLOCKS - 1:
            send(
                jnp.logical_and(sends_edge, sends_x),
                remote(
                    s_corner.at[1], r_corner.at[gy], ss_corner.at[1], rs_corner.at[gy],
                    gx + 1, gz, gz + 1,
                ),
            )
            send(
                sends_edge,
                remote(
                    s_edge.at[1], r_edge.at[gy], ss_edge.at[1], rs_edge.at[gy], gx, gz, gz + 1
                ),
            )

    pending.append((
        jnp.logical_and(sends_edge, sends_x),
        remote(s_corner.at[0], r_corner.at[gy], ss_corner.at[0], rs_corner.at[gy], gx + 1, gz + 1, 0),
    ))
    pending.append((
        jnp.logical_and(sends_edge, jnp.logical_not(edge_self)),
        remote(s_edge.at[0], r_edge.at[gy], ss_edge.at[0], rs_edge.at[gy], gx, gz + 1, 0),
    ))

    def arrive(when, buf, sems, c, source):
        @pl.when(when)
        def _():
            remote(source, buf.at[c], ss_main.at[0], sems.at[c], gx, gy, gz).wait_recv()

    for c in range(4):
        arrive(jnp.logical_not(main_self(c)), r_main, rs_main, c, s_main.at[0])
        arrive(jnp.logical_and(has_edge, jnp.logical_not(below_self(c))), r_edge, rs_edge, c, s_edge.at[0])
        arrive(has_x, r_x, rs_x, c, s_x.at[0])
        arrive(jnp.logical_and(has_x, has_edge), r_corner, rs_corner, c, s_corner.at[0])
    for n in range(6, 10):
        smalls[n].wait()

    top = sub8 == 0
    lane = iota((8, 128), 1)
    group = lane // 32
    lead = lax.rem(lane, 32) == 0

    def gathered(c, u):
        low_rows = (
            r_main[c, 16 * u : 16 * u + 8, :]
            + r_edge[c, 8 * u : 8 * u + 8, :]
            + jnp.where(top, r_x[c, 2 * u : 2 * u + 1, :] + r_corner[c, u : u + 1, :], 0.0)
        )
        high_rows = r_main[c, 16 * u + 8 : 16 * u + 16, :] + jnp.where(
            top, r_x[c, 2 * u + 1 : 2 * u + 2, :], 0.0
        )
        return low_rows, high_rows

    def by_group(values, shift):
        out = values[(0 - shift) % 4]
        for h in range(1, 4):
            out = jnp.where(group == h, values[(h - shift) % 4], out)
        return out

    extras = [gathered(c, CHUNKS) for c in range(4)]
    drive = {}
    for u in range(CHUNKS):
        mains = [gathered(c, u) for c in range(4)]
        for b in range(2):
            edges = [
                pltpu.roll(extras[c][b], 128 - u, axis=1) if u else extras[c][b] for c in range(4)
            ]
            edges = [jnp.where(lead, value, 0.0) for value in edges]
            for k in range(4):
                value = by_group([mains[c][b] for c in range(4)], k) + by_group(edges, k + 1)
                if k:
                    value = pltpu.roll(value, 128 - 32 * k, axis=1)
                drive[u // 2, 4 * (u % 2) + k, b] = value

    for b in range(2):
        bound, active = trop_v[:, b, :], tens_v[:, b, :]
        unbind, relax = unb_v[:, b, :], rel_v[:, b, :]
        for t in range(8):
            squared = drive[0, t, b] * drive[0, t, b]
            binding = squared / (squared + half_square)
            bound = bound + step_size * (bind_rate * binding * (1.0 - bound) - unbind * bound)
            active = active + step_size * relax * (peak_tension * drive[1, t, b] * bound - active)
        out_bound[:, b, :] = bound
        out_active[:, b, :] = active

    for when, copy in pending:
        @pl.when(when)
        def _():
            copy.wait_send()


def per_device(
    calcium, activation,
    element_first, offset_first, element_second, offset_second, element_third, offset_third,
    troponin, tension, unbind_rate, relax_rate,
):
    anywhere = pl.BlockSpec(memory_space=pl.ANY)
    vmem = pl.BlockSpec(memory_space=pltpu.VMEM)
    dma = pltpu.SemaphoreType.DMA
    small = jax.ShapeDtypeStruct(troponin.shape, f32)
    return pl.pallas_call(
        kernel,
        out_shape=(small, small),
        in_specs=[anywhere] * 12,
        out_specs=(vmem, vmem),
        scratch_shapes=[
            pltpu.VMEM((BLOCKS, CHUNKS, 4, 32, 8, 128), f32),
            pltpu.VMEM((2, 128), jnp.int32),
            pltpu.VMEM((2, 128), f32),
            pltpu.VMEM((4, 128), jnp.int32),
            pltpu.VMEM((4, 128), f32),
            pltpu.VMEM((1, 128), jnp.int32),
            pltpu.VMEM((1, 128), f32),
            *[pltpu.VMEM(troponin.shape, f32) for _ in range(4)],
            pltpu.VMEM((BLOCKS, 2 * ROWS, 256), bf16),
            pltpu.VMEM((512, 256), bf16),
            pltpu.VMEM((512, 256), bf16),
            pltpu.VMEM((BLOCKS, MAIN, 128), f32),
            pltpu.VMEM((BLOCKS, 16, 128), f32),
            pltpu.VMEM((2, EDGE, 128), f32),
            pltpu.VMEM((2, 8, 128), f32),
            pltpu.VMEM((4, MAIN, 128), f32),
            pltpu.VMEM((4, 16, 128), f32),
            pltpu.VMEM((4, EDGE, 128), f32),
            pltpu.VMEM((4, 8, 128), f32),
            dma((BLOCKS, CHUNKS)),
            dma((10,)),
            dma((BLOCKS,)),
            dma((BLOCKS,)),
            dma((2,)),
            dma((2,)),
            dma((4,)),
            dma((4,)),
            dma((4,)),
            dma((4,)),
        ],
        compiler_params=pltpu.CompilerParams(collective_id=0, has_side_effects=True),
        name="restrict_and_step",
    )(
        calcium, activation,
        element_first.reshape(2, 128), offset_first.reshape(2, 128),
        element_second.reshape(4, 128), offset_second.reshape(4, 128),
        element_third.reshape(1, 128), offset_third.reshape(1, 128),
        troponin, tension, unbind_rate, relax_rate,
    )


def solution(mesh):
    nodes = P("gx", ("gy", "gz"), None)
    fine = P(None, "gx", "gz", "gy")
    return jax.shard_map(
        per_device,
        mesh=mesh,
        in_specs=(fine, fine, P(), P(), P(), P(), P(), P(), nodes, nodes, nodes, nodes),
        out_specs=(nodes, nodes),
        check_vma=False,
    )
```

time: 76.9 us -> 18.5 us (0.24)
  blocking collectives: 26.1 us -> 0 us
  matrix products: 17.6 us -> 0 us
  Pallas kernels: 0 us -> 15.1 us
  waiting for transfers between devices: 10.7 us -> 0 us
  other arithmetic: 8.23 us -> 0 us
  starting transfers between devices: 8.2 us -> 0 us
  local copies, waits for them, and re-layouts: 4.72 us -> 2.59 us
    all_to_all x2 -> x0, blocking collectives: 26.1 us -> none  [the longest x1 15.1 us: per_device(): lax.all_to_all(lax.all_to_all(shaped, 'gz', split_axis=4, concat_axis=1,...]
    dot_general x6 -> x0, matrix products: 17.6 us -> none  [the longest x2 12.3 us: restrict_block(): section = jnp.einsum('ai,sizy->sazy', weight_row, field, precision=highest)]
    pallas_call x0 -> x1, Pallas kernels: none -> 15.1 us  [per_device(): pl.pallas_call(kernel, out_shape=(small, small), in_specs=[anywhere] * 12...]
    ppermute x3 -> x0, waiting for transfers between devices: 10.7 us -> none  [shifted(): return lax.ppermute(x, axis, pairs)]
    ppermute x3 -> x0, starting transfers between devices: 8.2 us -> none  [shifted(): return lax.ppermute(x, axis, pairs)]
    add x10 -> x0, other arithmetic: 2.33 us -> none  [the longest x3 2.02 us: axis_weights(): following = element[None, :] + 1 == node_ids[:, None]]
    sub x3 -> x0, other arithmetic: 2.02 us -> none  [axis_weights(): 1.0 - offset[None, :]]
    all_to_all x2 -> x0, other arithmetic: 1.96 us -> none  [the longest x1 0.98 us: per_device(): lax.all_to_all(lax.all_to_all(shaped, 'gz', split_axis=4, concat_axis=1,...]
  transfers between devices with their start and end apart: 3 -> 0, of which waited for: 3 -> 0; matrix products, arithmetic and copies ran while one was open for 0% -> 0% of each run, Pallas kernels for 0% -> 0%
where the time goes in v1:
time: 18.5 us; the launch traced here: 18.3 us
  Pallas kernels  15.1 us (82%)
  local copies, waits for them, and re-layouts  2.59 us (14%)
  between operations  0.64 us (3%)
    pallas_call x1, Pallas kernels, per_device(): pl.pallas_call(kernel, out_shape=(small, small), in_specs=[anywhere] * 12...  15.1 us
    unnamed x2, local copies, waits for them, and re-layouts  2.59 us

profile of v1, /device:TPU:64, one launch (start us, length us, event | category | flops | bytes accessed | tf_op | source)
XLA Modules:
  0.0 18.3 jit_solution(16060200289441857260)
XLA Ops:
  0.6 15.1 %restrict_and_step.1 = (f32[8,2,128]{2,1,0:T(2,128)}, f32[8,2,128]{2,1,0:T(2,128)}) custom-call(f32[8,32,32,128]{3,2,1,0:T(8,128)} %cal.1, f32[8,32,32,128]{3,2,1,0:T(8,128)} %act.1, s32[2,128]{1,0:T(2,128)} %bitcast.8, f32[2,128]{1,0:T(2,128)} %bitcast.9, s32[4,128]{1,0:T(4,128)} %bitcast.6, f32[4,128]{1,0:T(4,128)} %bitcast.7, s32[1,128]{1,0:T(1,128)} %bitcast.10, ...), custom_call_target="tpu_custom_call" | custom-call | tf_op jit(solution)/shard_map/restrict_and_step/pallas_call | solution.py:417
  15.7 1.3 %copy.16 = f32[8,2,128]{2,1,0:T(2,128)} copy(f32[8,2,128]{2,1,0:T(2,128)} %get-tuple-element.4) | data formatting | bytes 16384
  17.0 1.3 %copy.17 = f32[8,2,128]{2,1,0:T(2,128)} copy(f32[8,2,128]{2,1,0:T(2,128)} %get-tuple-element.5) | data formatting | bytes 16384

commit v2 on v1

--- a/solution.py
+++ b/solution.py
@@ -80,8 +80,20 @@
              (trop, trop_v), (tens, tens_v), (unb, unb_v), (rel, rel_v)]
         )
     ]
-    for copy in smalls:
+    barrier = pltpu.get_barrier_semaphore()
+
+    def ready(x, y, z):
+        pl.semaphore_signal(
+            barrier, inc=1, device_id={"gx": x, "gy": y, "gz": z}, device_id_type=MESH
+        )
+
+    for copy in smalls[:6]:
         copy.start()
+
+    @pl.when(gx > 0)
+    def _():
+        ready(gx - 1, 0, gy)
+
     loads = {}
     for j in range(BLOCKS):
         first_cell = pl.multiple_of(blocks[j] * 8, 8)
@@ -89,6 +101,8 @@
             src = (cal, act)[u // 2].at[pl.ds(4 * (u % 2), 4), :, pl.ds(first_cell, 8), :]
             loads[j, u] = pltpu.make_async_copy(src, x_buf.at[j, u], sem_x.at[j, u])
             loads[j, u].start()
+    for copy in smalls[6:]:
+        copy.start()
 
     from_below = jnp.logical_and(gz == 0, gy > 0)
     has_edge = jnp.logical_or(from_below, gz == gy + 1)
@@ -102,13 +116,6 @@
     def below_self(c):
         return jnp.logical_and(jnp.logical_and(gy == 1, gz == 0), gy == c)
 
-    barrier = pltpu.get_barrier_semaphore()
-
-    def ready(x, y, z):
-        pl.semaphore_signal(
-            barrier, inc=1, device_id={"gx": x, "gy": y, "gz": z}, device_id_type=MESH
-        )
-
     for c in range(4):
         @pl.when(jnp.logical_not(main_self(c)))
         def _():
@@ -118,9 +125,10 @@
         def _():
             ready(gx, c, gy - 1)
 
-        @pl.when(has_x)
-        def _():
-            ready(gx - 1, c, gy)
+        if c > 0:
+            @pl.when(has_x)
+            def _():
+                ready(gx - 1, c, gy)
 
         @pl.when(jnp.logical_and(has_x, from_below))
         def _():
@@ -224,6 +232,7 @@
         ys = []
         for u in range(CHUNKS):
             loads[j, u].wait()
+        for u in range(CHUNKS):
             halves = []
             for pair in range(2):
                 x = jnp.concatenate(
@@ -405,18 +414,30 @@
             copy.wait_send()
 
 
+def write_out(bound, active, out_bound, out_active, sems):
+    copies = [
+        pltpu.make_async_copy(bound, out_bound, sems.at[0]),
+        pltpu.make_async_copy(active, out_active, sems.at[1]),
+    ]
+    for copy in copies:
+        copy.start()
+    for copy in copies:
+        copy.wait()
+
+
 def per_device(
     calcium, activation,
     element_first, offset_first, element_second, offset_second, element_third, offset_third,
     troponin, tension, unbind_rate, relax_rate,
 ):
-    anywhere = pl.BlockSpec(memory_space=pl.ANY)
+    anywhere = pl.BlockSpec(memory_space=pltpu.HBM)
     vmem = pl.BlockSpec(memory_space=pltpu.VMEM)
     dma = pltpu.SemaphoreType.DMA
     small = jax.ShapeDtypeStruct(troponin.shape, f32)
-    return pl.pallas_call(
+    kept = pltpu.VMEM(troponin.shape, f32)
+    bound, active = pl.pallas_call(
         kernel,
-        out_shape=(small, small),
+        out_shape=(kept, kept),
         in_specs=[anywhere] * 12,
         out_specs=(vmem, vmem),
         scratch_shapes=[
@@ -450,7 +471,9 @@
             dma((4,)),
             dma((4,)),
         ],
-        compiler_params=pltpu.CompilerParams(collective_id=0, has_side_effects=True),
+        compiler_params=pltpu.CompilerParams(
+            collective_id=0, has_side_effects=True, vmem_limit_bytes=60 * 1024 * 1024
+        ),
         name="restrict_and_step",
     )(
         calcium, activation,
@@ -459,6 +482,15 @@
         element_third.reshape(1, 128), offset_third.reshape(1, 128),
         troponin, tension, unbind_rate, relax_rate,
     )
+    return pl.pallas_call(
+        write_out,
+        out_shape=(small, small),
+        in_specs=[vmem, vmem],
+        out_specs=(anywhere, anywhere),
+        scratch_shapes=[dma((2,))],
+        compiler_params=pltpu.CompilerParams(vmem_limit_bytes=2**20),
+        name="write_out",
+    )(bound, active)
 
 
 def solution(mesh):

time: 18.5 us -> 14.7 us (0.79)
  local copies, waits for them, and re-layouts: 2.59 us -> 0 us
  Pallas kernels: 15.1 us -> 13.9 us
    unnamed x2 -> x0, local copies, waits for them, and re-layouts: 2.59 us -> none
    pallas_call x1 -> x2, Pallas kernels: 15.1 us -> 13.9 us  [the longest x1 13.3 us: per_device(): pl.pallas_call(kernel, out_shape=(kept, kept), in_specs=[anywhere] * 12,...]
where the time goes in v2:
time: 14.7 us; the launch traced here: 14.6 us
  Pallas kernels  13.9 us (95%)
  between operations  0.64 us (4%)
    pallas_call x1, Pallas kernels, per_device(): pl.pallas_call(kernel, out_shape=(kept, kept), in_specs=[anywhere] * 12,...  13.3 us
    pallas_call x1, Pallas kernels, per_device(): pl.pallas_call(write_out, out_shape=(small, small), in_specs=[vmem, vmem]...  0.62 us

profile of v2, /device:TPU:64, one launch (start us, length us, event | category | flops | bytes accessed | tf_op | source)
XLA Modules:
  0.0 14.6 jit_solution(12254785779298955310)
XLA Ops:
  0.6 13.3 %restrict_and_step.1 = (f32[8,2,128]{2,1,0:T(2,128)S(1)}, f32[8,2,128]{2,1,0:T(2,128)S(1)}) custom-call(f32[8,32,32,128]{3,2,1,0:T(8,128)} %cal.1, f32[8,32,32,128]{3,2,1,0:T(8,128)} %act.1, s32[2,128]{1,0:T(2,128)} %bitcast.8, f32[2,128]{1,0:T(2,128)} %bitcast.9, s32[4,128]{1,0:T(4,128)} %bitcast.6, f32[4,128]{1,0:T(4,128)} %bitcast.7, s32[1,128]{1,0:T(1,128)} %bitcast.10, ...), custom_call_target="tpu_custom_call" | custom-call | tf_op jit(solution)/shard_map/restrict_and_step/pallas_call | solution.py:438
  14.0 0.6 %write_out.1 = (f32[8,2,128]{2,1,0:T(2,128)}, f32[8,2,128]{2,1,0:T(2,128)}) custom-call(f32[8,2,128]{2,1,0:T(2,128)S(1)} %get-tuple-element.4.bound, f32[8,2,128]{2,1,0:T(2,128)S(1)} %get-tuple-element.5.active), custom_call_target="tpu_custom_call" | custom-call | tf_op jit(solution)/shard_map/write_out/pallas_call | solution.py:485

commit v3 on v2

--- a/solution.py
+++ b/solution.py
@@ -19,6 +19,7 @@
 BLOCKS = 4
 ROWS = 32
 CHUNKS = 4
+ORDER = (3, 0, 1, 2)
 MAIN = CHUNKS * 16 + 16
 EDGE = CHUNKS * 8 + 8
 
@@ -62,7 +63,7 @@
     cal, act, ef, of, es, os_, et, ot, trop, tens, unb, rel,
     out_bound, out_active,
     x_buf, ef_v, of_v, es_v, os_v, et_v, ot_v, trop_v, tens_v, unb_v, rel_v,
-    w1, w2h, w2l,
+    w1, w2h, w2l, y_buf, tail, extra_buf,
     s_main, s_x, s_edge, s_corner,
     r_main, r_x, r_edge, r_corner,
     sem_x, sem_small,
@@ -71,7 +72,7 @@
 ):
     gx, gy, gz = lax.axis_index("gx"), lax.axis_index("gy"), lax.axis_index("gz")
     last_x = lax.axis_size("gx") - 1
-    blocks = [lax.rem(gz + 1 + j, BLOCKS) for j in range(BLOCKS)]
+    blocks = ORDER
 
     smalls = [
         pltpu.make_async_copy(src, dst, sem_small.at[n])
@@ -87,53 +88,62 @@
             barrier, inc=1, device_id={"gx": x, "gy": y, "gz": z}, device_id_type=MESH
         )
 
+    from_below = jnp.logical_and(gz == 0, gy > 0)
+    has_edge = jnp.logical_or(from_below, gz == SLABS - 1)
+    has_x = gx > 0
+    sends_x = gx < last_x
+    sends_edge = gz < SLABS - 1
+
+    for c in range(4):
+        @pl.when(has_x)
+        def _():
+            ready(gx - 1, c, gy)
+
+        @pl.when(jnp.logical_and(has_x, from_below))
+        def _():
+            ready(gx - 1, c, gy - 1)
+
     for copy in smalls[:6]:
         copy.start()
 
-    @pl.when(gx > 0)
-    def _():
-        ready(gx - 1, 0, gy)
+    @pl.when(jnp.logical_or(gy != gz, gy != 0))
+    def _():
+        ready(gx, 0, gy)
 
     loads = {}
     for j in range(BLOCKS):
-        first_cell = pl.multiple_of(blocks[j] * 8, 8)
+        first_cell = blocks[j] * 8
         for u in range(CHUNKS):
             src = (cal, act)[u // 2].at[pl.ds(4 * (u % 2), 4), :, pl.ds(first_cell, 8), :]
             loads[j, u] = pltpu.make_async_copy(src, x_buf.at[j, u], sem_x.at[j, u])
+
+    def issue(j):
+        for u in range(CHUNKS):
             loads[j, u].start()
+
+    issue(0)
     for copy in smalls[6:]:
         copy.start()
 
-    from_below = jnp.logical_and(gz == 0, gy > 0)
-    has_edge = jnp.logical_or(from_below, gz == gy + 1)
-    has_x = gx > 0
-    sends_x = gx < last_x
-    sends_edge = gz < SLABS - 1
-
     def main_self(c):
         return jnp.logical_and(gy == gz, gy == c)
 
     def below_self(c):
         return jnp.logical_and(jnp.logical_and(gy == 1, gz == 0), gy == c)
 
+    last_self = jnp.logical_and(gy == SLABS - 1, gz == SLABS - 1)
+
     for c in range(4):
-        @pl.when(jnp.logical_not(main_self(c)))
-        def _():
-            ready(gx, c, gy)
+        if c > 0:
+            @pl.when(jnp.logical_not(main_self(c)))
+            def _():
+                ready(gx, c, gy)
 
         @pl.when(jnp.logical_and(from_below, jnp.logical_not(below_self(c))))
         def _():
             ready(gx, c, gy - 1)
 
-        if c > 0:
-            @pl.when(has_x)
-            def _():
-                ready(gx - 1, c, gy)
-
-        @pl.when(jnp.logical_and(has_x, from_below))
-        def _():
-            ready(gx - 1, c, gy - 1)
-
+    issue(1)
     edge_self = jnp.logical_and(gz == 0, gy == 1)
     expected = (
         jnp.where(gy == gz, 3, 4)
@@ -162,6 +172,7 @@
     pick_cell = iota((128, 256), 0) - lax.rem(iota((128, 256), 1), 8)
     for n in range(4):
         smalls[n].wait()
+    issue(2)
     e_first = jnp.concatenate([ef_v[0:1, :], ef_v[1:2, :]], axis=1)
     o_first = jnp.concatenate([of_v[0:1, :], of_v[1:2, :]], axis=1)
     node_first = 8 * gx + a_of
@@ -180,34 +191,37 @@
         w1[j, 0:ROWS] = high
         w1[j, ROWS:] = low
 
+    issue(3)
     smalls[4].wait()
     smalls[5].wait()
-    node_row = iota((40, 1), 0)
-    node_second = 32 * gy + node_row
-    inside = jnp.logical_and(node_row < 33, node_second < 128)
-    total = jnp.zeros((40, 1), f32)
-    for n in range(4):
-        total += jnp.sum(
-            raw_weights(es_v[n : n + 1, :], os_v[n : n + 1, :], node_second), axis=1, keepdims=True
-        )
-    own = raw_weights(es_v[pl.ds(gy, 1), :], os_v[pl.ds(gy, 1), :], node_second)
-    own = jnp.where(inside, own / jnp.where(inside, total, 1.0), 0.0)
-    lane_w = iota((128, 128), 1)
-    turned = jnp.transpose(jnp.concatenate([own[0:32]] * 4, axis=0))
-    turned_edge = jnp.transpose(jnp.broadcast_to(own[32:33], (128, 128)))
-    for k in range(4):
-        group = lax.rem(gy + k, 4)
-        edge_lane = 32 * lax.rem(gy + 1 + k, 4)
-        wide = jnp.concatenate(
-            [
-                jnp.where(lane_w // 32 == group, turned, 0.0),
-                jnp.where(lane_w == edge_lane, turned_edge, 0.0),
-            ],
-            axis=1,
-        )
-        high, low = split(wide)
-        w2h[128 * k : 128 * (k + 1), :] = high
-        w2l[128 * k : 128 * (k + 1), :] = low
+
+    def second_weights():
+        node_row = iota((40, 1), 0)
+        node_second = 32 * gy + node_row
+        inside = jnp.logical_and(node_row < 33, node_second < 128)
+        total = jnp.zeros((40, 1), f32)
+        for n in range(4):
+            total += jnp.sum(
+                raw_weights(es_v[n : n + 1, :], os_v[n : n + 1, :], node_second), axis=1, keepdims=True
+            )
+        own = raw_weights(es_v[pl.ds(gy, 1), :], os_v[pl.ds(gy, 1), :], node_second)
+        own = jnp.where(inside, own / jnp.where(inside, total, 1.0), 0.0)
+        lane_w = iota((128, 128), 1)
+        turned = jnp.transpose(jnp.concatenate([own[0:32]] * 4, axis=0))
+        turned_edge = jnp.transpose(jnp.broadcast_to(own[32:33], (128, 128)))
+        for k in range(4):
+            group = lax.rem(gy + k, 4)
+            edge_lane = 32 * lax.rem(gy + 1 + k, 4)
+            wide = jnp.concatenate(
+                [
+                    jnp.where(lane_w // 32 == group, turned, 0.0),
+                    jnp.where(lane_w == edge_lane, turned_edge, 0.0),
+                ],
+                axis=1,
+            )
+            high, low = split(wide)
+            w2h[128 * k : 128 * (k + 1), :] = high
+            w2l[128 * k : 128 * (k + 1), :] = low
 
     def remote(src, dst, send_sem, recv_sem, x, y, z):
         return pltpu.make_async_remote_copy(
@@ -215,137 +229,138 @@
             device_id={"gx": x, "gy": y, "gz": z}, device_id_type=MESH,
         )
 
-    pending = []
-
-    def send(when, copy):
-        @pl.when(when)
-        def _():
-            copy.start()
-
-        pending.append((when, copy))
-
-    always = gx >= 0
+    copies = {}
+
+    def put(name, block, when, copy):
+        rank = {"x": 1, "corner": 2, "edge": 3, "main": 4}[name]
+        copies.setdefault(block, []).append((rank, when, copy))
+
     sub8 = iota((8, 128), 0)
-    carry = None
-    for j in range(BLOCKS):
-        block = blocks[j]
-        ys = []
-        for u in range(CHUNKS):
-            loads[j, u].wait()
-        for u in range(CHUNKS):
-            halves = []
+
+    def first_stage(j, f):
+        slot = (2 * j + f) % 2
+        for n in range(2):
+            u = 2 * f + n
             for pair in range(2):
                 x = jnp.concatenate(
-                    [x_buf[j, u, 2 * pair + n].reshape(256, 128) for n in range(2)], axis=1
+                    [x_buf[j, u, 2 * pair + m].reshape(256, 128) for m in range(2)], axis=1
                 )
                 high, low = split(x)
-                both = dot(w1[j], high)
-                halves.append(both[0:ROWS] + both[ROWS:] + dot(w1[j, 0:ROWS], low))
-            ys.append(jnp.concatenate(halves, axis=1))
-        y = jnp.concatenate(ys, axis=0)
-        high, low = split(y)
-        n = CHUNKS * ROWS
-        both = dot(jnp.concatenate([high, low], axis=0), w2h[...])
-        z = both[0:n] + both[n:] + dot(high, w2l[...])
-        parts = [z[ROWS * u : ROWS * (u + 1), 0:128] for u in range(CHUNKS)]
-        extra = z[0:ROWS, 128:256]
-        for u in range(1, CHUNKS):
-            extra += pltpu.roll(z[ROWS * u : ROWS * (u + 1), 128:256], u, axis=1)
-        parts.append(extra)
-        if carry is not None:
-            use = block != 0
-            merged = []
-            for part, (rows8, corner) in zip(parts, carry):
-                merged.append(
-                    jnp.concatenate(
-                        [
-                            part[0:8] + jnp.where(use, rows8, 0.0),
-                            part[8:24],
-                            part[24:32] + jnp.where(jnp.logical_and(use, sub8 == 0), corner, 0.0),
-                        ],
-                        axis=0,
-                    )
-                )
-            parts = merged
-        carry = [(part[16:24], pltpu.roll(part[24:32], 6, axis=0)) for part in parts]
-        for u in range(CHUNKS + 1):
-            s_main[j, 16 * u : 16 * (u + 1), :] = parts[u][0:16]
-            s_x[j, 2 * u : 2 * (u + 1), :] = parts[u][24:26]
-
-        def store_edge(slot):
-            for u in range(CHUNKS + 1):
-                s_edge[slot, 8 * u : 8 * (u + 1), :] = parts[u][16:24]
-                s_corner[slot, u : u + 1, :] = parts[u][26:27]
-
-        up = jnp.logical_and(block == BLOCKS - 1, sends_edge)
-
-        @pl.when(up)
+                twice = dot(w1[j], high)
+                y = twice[0:ROWS] + twice[ROWS:] + dot(w1[j, 0:ROWS], low)
+                high, low = split(y)
+                columns = slice(256 * pair, 256 * (pair + 1))
+                y_buf[slot, ROWS * n : ROWS * (n + 1), columns] = high
+                y_buf[slot, ROWS * (2 + n) : ROWS * (3 + n), columns] = low
+
+    def finish(j, u, part):
+        if blocks[j] > 0 and j > 0:
+            corner = pltpu.roll(tail[u, 8:16, :], 6, axis=0)
+            part = [
+                part[0:8] + tail[u, 0:8, :],
+                part[8:16],
+                part[16:24],
+                part[24:32] + jnp.where(sub8 == 0, corner, 0.0),
+            ]
+        else:
+            part = [part[8 * n : 8 * (n + 1)] for n in range(4)]
+        if j < BLOCKS - 1:
+            tail[u, 0:8, :] = part[2]
+            tail[u, 8:16, :] = part[3]
+        s_main[j, 16 * u : 16 * u + 8, :] = part[0]
+        s_main[j, 16 * u + 8 : 16 * u + 16, :] = part[1]
+        s_x[j, 2 * u : 2 * (u + 1), :] = part[3][0:2]
+        if j in (0, BLOCKS - 1):
+            slot = 0 if j == 0 else 1
+            s_edge[slot, 8 * u : 8 * (u + 1), :] = part[2]
+            s_corner[slot, u : u + 1, :] = part[3][2:3]
+
+    def second_stage(j, f):
+        y = y_buf[(2 * j + f) % 2]
+        twice = dot(y, w2h[...])
+        n = 2 * ROWS
+        z = twice[0:n] + twice[n:] + dot(y[0:n], w2l[...])
+        extra = 0.0 if f == 0 else extra_buf[...]
+        for n in range(2):
+            u = 2 * f + n
+            rows = z[ROWS * n : ROWS * (n + 1)]
+            finish(j, u, rows[:, 0:128])
+            extra += pltpu.roll(rows[:, 128:256], u, axis=1) if u else rows[:, 128:256]
+        if f == 0:
+            extra_buf[...] = extra
+        else:
+            finish(j, CHUNKS, extra)
+
+    both = jnp.logical_and
+    for j, block in enumerate(blocks):
+        put("x", j, sends_x, remote(
+            s_x.at[j], r_x.at[gy], ss_x.at[j], rs_x.at[gy], gx + 1, gz, block))
+        if j == 0:
+            put("corner", j, both(sends_edge, sends_x), remote(
+                s_corner.at[0], r_corner.at[gy], ss_corner.at[0], rs_corner.at[gy],
+                gx + 1, gz + 1, 0))
+            put("edge", j, both(sends_edge, jnp.logical_not(edge_self)), remote(
+                s_edge.at[0], r_edge.at[gy], ss_edge.at[0], rs_edge.at[gy], gx, gz + 1, 0))
+        put("main", j, jnp.logical_not(both(gy == gz, gz == block)), remote(
+            s_main.at[j], r_main.at[gy], ss_main.at[j], rs_main.at[gy], gx, gz, block))
+        if j == BLOCKS - 1:
+            put("corner", j, sends_x, remote(
+                s_corner.at[1], r_corner.at[gy], ss_corner.at[1], rs_corner.at[gy],
+                gx + 1, gz, BLOCKS - 1))
+            put("edge", j, jnp.logical_not(last_self), remote(
+                s_edge.at[1], r_edge.at[gy], ss_edge.at[1], rs_edge.at[gy],
+                gx, gz, BLOCKS - 1))
+
+    def send_blocks(js, when=None):
+        ordered = [pair for j in js for pair in copies[j]]
+        for _, condition, copy in sorted(ordered, key=lambda pair: pair[0]):
+            condition = condition if when is None else both(condition, when)
+
+            @pl.when(condition)
+            def _():
+                copy.start()
+
+    late = gz == 0
+    early = jnp.logical_not(late)
+    EARLY = 4
+    for h in range(2 * BLOCKS):
+        j, f = h // 2, h % 2
+        for u in range(2 * f, 2 * f + 2):
+            loads[j, u].wait()
+        if h == 0:
+            second_weights()
+        else:
+            second_stage((h - 1) // 2, (h - 1) % 2)
+        first_stage(j, f)
+        if h == EARLY:
+            @pl.when(early)
+            def _():
+                pl.semaphore_wait(barrier, expected)
+
+            send_blocks(range(j), early)
+        elif h > EARLY and f == 0:
+            send_blocks([j - 1], early)
+    second_stage(BLOCKS - 1, 1)
+
+    @pl.when(late)
+    def _():
+        pl.semaphore_wait(barrier, expected)
+
+    send_blocks(range(BLOCKS - 1), late)
+    send_blocks([BLOCKS - 1])
+
+    for j, block in enumerate(blocks):
+        @pl.when(both(gy == gz, gz == block))
         def _():
-            store_edge(0)
-
-        if j == BLOCKS - 1:
-            @pl.when(sends_edge)
-            def _():
-                store_edge(1)
-
-        if j == 0:
-            pl.semaphore_wait(barrier, expected)
-
-        send(
-            sends_x,
-            remote(s_x.at[j], r_x.at[gy], ss_x.at[j], rs_x.at[gy], gx + 1, gz, block),
-        )
-        main_copy = remote(
-            s_main.at[j], r_main.at[gy], ss_main.at[j], rs_main.at[gy], gx, gz, block
-        )
-        if j < BLOCKS - 1:
-            send(always, main_copy)
-        else:
-            send(gy != gz, main_copy)
-
-            @pl.when(gy == gz)
-            def _():
-                r_main[pl.ds(gy, 1)] = s_main[pl.ds(j, 1)]
-
-        @pl.when(jnp.logical_and(up, sends_x))
-        def _():
-            remote(
-                s_corner.at[0], r_corner.at[gy], ss_corner.at[0], rs_corner.at[gy], gx + 1, gz + 1, 0
-            ).start()
-
-        @pl.when(jnp.logical_and(up, jnp.logical_not(edge_self)))
-        def _():
-            remote(
-                s_edge.at[0], r_edge.at[gy], ss_edge.at[0], rs_edge.at[gy], gx, gz + 1, 0
-            ).start()
-
-        @pl.when(jnp.logical_and(up, edge_self))
-        def _():
-            r_edge[pl.ds(gy, 1)] = s_edge[0:1]
-
-        if j == BLOCKS - 1:
-            send(
-                jnp.logical_and(sends_edge, sends_x),
-                remote(
-                    s_corner.at[1], r_corner.at[gy], ss_corner.at[1], rs_corner.at[gy],
-                    gx + 1, gz, gz + 1,
-                ),
-            )
-            send(
-                sends_edge,
-                remote(
-                    s_edge.at[1], r_edge.at[gy], ss_edge.at[1], rs_edge.at[gy], gx, gz, gz + 1
-                ),
-            )
-
-    pending.append((
-        jnp.logical_and(sends_edge, sends_x),
-        remote(s_corner.at[0], r_corner.at[gy], ss_corner.at[0], rs_corner.at[gy], gx + 1, gz + 1, 0),
-    ))
-    pending.append((
-        jnp.logical_and(sends_edge, jnp.logical_not(edge_self)),
-        remote(s_edge.at[0], r_edge.at[gy], ss_edge.at[0], rs_edge.at[gy], gx, gz + 1, 0),
-    ))
+            r_main[pl.ds(gy, 1)] = s_main[j : j + 1]
+
+    @pl.when(both(sends_edge, edge_self))
+    def _():
+        r_edge[pl.ds(gy, 1)] = s_edge[0:1]
+
+    @pl.when(last_self)
+    def _():
+        r_edge[pl.ds(gy, 1)] = s_edge[1:2]
 
     def arrive(when, buf, sems, c, source):
         @pl.when(when)
@@ -354,7 +369,7 @@
 
     for c in range(4):
         arrive(jnp.logical_not(main_self(c)), r_main, rs_main, c, s_main.at[0])
-        arrive(jnp.logical_and(has_edge, jnp.logical_not(below_self(c))), r_edge, rs_edge, c, s_edge.at[0])
+        arrive(jnp.logical_and(has_edge, jnp.logical_not(jnp.logical_or(below_self(c), both(last_self, gy == c)))), r_edge, rs_edge, c, s_edge.at[0])
         arrive(has_x, r_x, rs_x, c, s_x.at[0])
         arrive(jnp.logical_and(has_x, has_edge), r_corner, rs_corner, c, s_corner.at[0])
     for n in range(6, 10):
@@ -400,18 +415,22 @@
     for b in range(2):
         bound, active = trop_v[:, b, :], tens_v[:, b, :]
         unbind, relax = unb_v[:, b, :], rel_v[:, b, :]
+        keep_bound = 1.0 - step_size * unbind
+        keep_active = 1.0 - step_size * relax
         for t in range(8):
             squared = drive[0, t, b] * drive[0, t, b]
-            binding = squared / (squared + half_square)
-            bound = bound + step_size * (bind_rate * binding * (1.0 - bound) - unbind * bound)
-            active = active + step_size * relax * (peak_tension * drive[1, t, b] * bound - active)
+            gain = (step_size * bind_rate) * (squared / (squared + half_square))
+            pull = (step_size * peak_tension) * relax * drive[1, t, b]
+            bound = bound * (keep_bound - gain) + gain
+            active = active * keep_active + pull * bound
         out_bound[:, b, :] = bound
         out_active[:, b, :] = active
 
-    for when, copy in pending:
-        @pl.when(when)
-        def _():
-            copy.wait_send()
+    for j in range(BLOCKS):
+        for _, when, copy in copies[j]:
+            @pl.when(when)
+            def _():
+                copy.wait_send()
 
 
 def write_out(bound, active, out_bound, out_active, sems):
@@ -452,6 +471,9 @@
             pltpu.VMEM((BLOCKS, 2 * ROWS, 256), bf16),
             pltpu.VMEM((512, 256), bf16),
             pltpu.VMEM((512, 256), bf16),
+            pltpu.VMEM((2, 4 * ROWS, 512), bf16),
+            pltpu.VMEM((CHUNKS + 1, 16, 128), f32),
+            pltpu.VMEM((ROWS, 128), f32),
             pltpu.VMEM((BLOCKS, MAIN, 128), f32),
             pltpu.VMEM((BLOCKS, 16, 128), f32),
             pltpu.VMEM((2, EDGE, 128), f32),

time: 14.7 us -> 13.2 us (0.90)
  the two profiles are of different devices: /device:TPU:64 before, /device:TPU:97 now
where the time goes in v3:
time: 13.2 us; the launch traced here: 13.1 us
  Pallas kernels  12.4 us (94%)
  between operations  0.64 us (5%)
    pallas_call x1, Pallas kernels, per_device(): pl.pallas_call(kernel, out_shape=(kept, kept), in_specs=[anywhere] * 12,...  11.8 us
    pallas_call x1, Pallas kernels, per_device(): pl.pallas_call(write_out, out_shape=(small, small), in_specs=[vmem, vmem]...  0.62 us

profile of v3, /device:TPU:97, one launch (start us, length us, event | category | flops | bytes accessed | tf_op | source)
XLA Modules:
  0.0 13.1 jit_solution(8905155749015322653)
XLA Ops:
  0.6 11.8 %restrict_and_step.1 = (f32[8,2,128]{2,1,0:T(2,128)S(1)}, f32[8,2,128]{2,1,0:T(2,128)S(1)}) custom-call(f32[8,32,32,128]{3,2,1,0:T(8,128)} %cal.1, f32[8,32,32,128]{3,2,1,0:T(8,128)} %act.1, s32[2,128]{1,0:T(2,128)} %bitcast.8, f32[2,128]{1,0:T(2,128)} %bitcast.9, s32[4,128]{1,0:T(4,128)} %bitcast.6, f32[4,128]{1,0:T(4,128)} %bitcast.7, s32[1,128]{1,0:T(1,128)} %bitcast.10, ...), custom_call_target="tpu_custom_call" | custom-call | tf_op jit(solution)/shard_map/restrict_and_step/pallas_call | solution.py:457
  12.4 0.6 %write_out.1 = (f32[8,2,128]{2,1,0:T(2,128)}, f32[8,2,128]{2,1,0:T(2,128)}) custom-call(f32[8,2,128]{2,1,0:T(2,128)S(1)} %get-tuple-element.4.bound, f32[8,2,128]{2,1,0:T(2,128)S(1)} %get-tuple-element.5.active), custom_call_target="tpu_custom_call" | custom-call | tf_op jit(solution)/shard_map/write_out/pallas_call | solution.py:507

commit v4 on v3

--- a/solution.py
+++ b/solution.py
@@ -20,6 +20,7 @@
 ROWS = 32
 CHUNKS = 4
 ORDER = (3, 0, 1, 2)
+PLACE = (4, 4, 4, 4, 4, 4)
 MAIN = CHUNKS * 16 + 16
 EDGE = CHUNKS * 8 + 8
 
@@ -68,7 +69,7 @@
     r_main, r_x, r_edge, r_corner,
     sem_x, sem_small,
     ss_main, ss_x, ss_edge, ss_corner,
-    rs_main, rs_x, rs_edge, rs_corner,
+    rs_main, rs_x, rs_edge, rs_corner, x_ready,
 ):
     gx, gy, gz = lax.axis_index("gx"), lax.axis_index("gy"), lax.axis_index("gz")
     last_x = lax.axis_size("gx") - 1
@@ -94,14 +95,26 @@
     sends_x = gx < last_x
     sends_edge = gz < SLABS - 1
 
+    near = gz < 2
+    relays = jnp.logical_and(gz >= 2, sends_x)
+
     for c in range(4):
-        @pl.when(has_x)
+        @pl.when(jnp.logical_and(has_x, near))
         def _():
             ready(gx - 1, c, gy)
 
         @pl.when(jnp.logical_and(has_x, from_below))
         def _():
             ready(gx - 1, c, gy - 1)
+
+    @pl.when(jnp.logical_and(has_x, gz >= 2))
+    def _():
+        ready(gx - 1, gy, gz)
+
+    for q in (2, 3):
+        @pl.when(jnp.logical_and(sends_x, jnp.logical_not(jnp.logical_and(gy == gz, gz == q))))
+        def _():
+            ready(gx, gz, q)
 
     for copy in smalls[:6]:
         copy.start()
@@ -147,7 +160,8 @@
     edge_self = jnp.logical_and(gz == 0, gy == 1)
     expected = (
         jnp.where(gy == gz, 3, 4)
-        + jnp.where(sends_x, 4, 0)
+        + jnp.where(sends_x, 2, 0)
+        + jnp.where(relays, jnp.where(gy == gz, 4, 5), 0)
         + jnp.where(jnp.logical_and(sends_edge, jnp.logical_not(edge_self)), 1, 0)
         + jnp.where(jnp.logical_and(sends_edge, sends_x), 1, 0)
     )
@@ -229,12 +243,6 @@
             device_id={"gx": x, "gy": y, "gz": z}, device_id_type=MESH,
         )
 
-    copies = {}
-
-    def put(name, block, when, copy):
-        rank = {"x": 1, "corner": 2, "edge": 3, "main": 4}[name]
-        copies.setdefault(block, []).append((rank, when, copy))
-
     sub8 = iota((8, 128), 0)
 
     def first_stage(j, f):
@@ -292,62 +300,87 @@
             finish(j, CHUNKS, extra)
 
     both = jnp.logical_and
+    copies = {}
     for j, block in enumerate(blocks):
-        put("x", j, sends_x, remote(
+        copies["x", j] = (sends_x, remote(
             s_x.at[j], r_x.at[gy], ss_x.at[j], rs_x.at[gy], gx + 1, gz, block))
         if j == 0:
-            put("corner", j, both(sends_edge, sends_x), remote(
+            copies["corner", 0] = (both(sends_edge, sends_x), remote(
                 s_corner.at[0], r_corner.at[gy], ss_corner.at[0], rs_corner.at[gy],
                 gx + 1, gz + 1, 0))
-            put("edge", j, both(sends_edge, jnp.logical_not(edge_self)), remote(
+            copies["edge", 0] = (both(sends_edge, jnp.logical_not(edge_self)), remote(
                 s_edge.at[0], r_edge.at[gy], ss_edge.at[0], rs_edge.at[gy], gx, gz + 1, 0))
-        put("main", j, jnp.logical_not(both(gy == gz, gz == block)), remote(
+        copies["main", j] = (jnp.logical_not(both(gy == gz, gz == block)), remote(
             s_main.at[j], r_main.at[gy], ss_main.at[j], rs_main.at[gy], gx, gz, block))
         if j == BLOCKS - 1:
-            put("corner", j, sends_x, remote(
+            copies["corner", 1] = (sends_x, remote(
                 s_corner.at[1], r_corner.at[gy], ss_corner.at[1], rs_corner.at[gy],
                 gx + 1, gz, BLOCKS - 1))
-            put("edge", j, jnp.logical_not(last_self), remote(
+            copies["edge", 1] = (jnp.logical_not(last_self), remote(
                 s_edge.at[1], r_edge.at[gy], ss_edge.at[1], rs_edge.at[gy],
                 gx, gz, BLOCKS - 1))
 
-    def send_blocks(js, when=None):
-        ordered = [pair for j in js for pair in copies[j]]
-        for _, condition, copy in sorted(ordered, key=lambda pair: pair[0]):
+    READY = [
+        [("corner", 0), ("edge", 0), ("main", 0)],
+        [("x", 1), ("main", 1)],
+        [("x", 2), ("main", 2)],
+        [("main", 3), ("edge", 1)],
+    ]
+    RANK = {"x": 0, "corner": 1, "edge": 2, "main": 3}
+
+    def send(names, when=None):
+        for name in names:
+            condition, copy = copies[name]
             condition = condition if when is None else both(condition, when)
 
             @pl.when(condition)
             def _():
                 copy.start()
 
-    late = gz == 0
-    early = jnp.logical_not(late)
-    EARLY = 4
-    for h in range(2 * BLOCKS):
+    def enter(when):
+        @pl.when(when)
+        def _():
+            pl.semaphore_wait(barrier, expected)
+
+        for c in range(4):
+            @pl.when(both(both(when, relays), jnp.logical_not(main_self(c))))
+            def _():
+                pl.semaphore_signal(
+                    x_ready.at[lax.max(gz - 2, 0)], inc=1,
+                    device_id={"gx": gx, "gy": c, "gz": gy}, device_id_type=MESH,
+                )
+
+        @pl.when(both(both(when, relays), gy == gz))
+        def _():
+            pl.semaphore_signal(x_ready.at[lax.max(gz - 2, 0)], inc=1)
+
+    place = jnp.where(gx == 3, jnp.where(gz == 2, PLACE[5], PLACE[4]), jnp.where(
+        gz == 0, PLACE[0], jnp.where(gz == 1, PLACE[1], jnp.where(gz == 2, PLACE[2], PLACE[3]))))
+    for h in range(2 * BLOCKS + 1):
         j, f = h // 2, h % 2
-        for u in range(2 * f, 2 * f + 2):
-            loads[j, u].wait()
+        if h < 2 * BLOCKS:
+            for u in range(2 * f, 2 * f + 2):
+                loads[j, u].wait()
         if h == 0:
             second_weights()
         else:
             second_stage((h - 1) // 2, (h - 1) % 2)
-        first_stage(j, f)
-        if h == EARLY:
-            @pl.when(early)
-            def _():
-                pl.semaphore_wait(barrier, expected)
-
-            send_blocks(range(j), early)
-        elif h > EARLY and f == 0:
-            send_blocks([j - 1], early)
-    second_stage(BLOCKS - 1, 1)
-
-    @pl.when(late)
-    def _():
-        pl.semaphore_wait(barrier, expected)
-
-    send_blocks(range(BLOCKS - 1), late)
-    send_blocks([BLOCKS - 1])
+        if h < 2 * BLOCKS:
+            first_stage(j, f)
+        if h in PLACE:
+            here = place == h
+            enter(here)
+            names = [name for i in range(j - 1) for name in READY[i]]
+            send(sorted(names, key=lambda name: RANK[name[0]]), here)
+        if h >= min(PLACE) and f == 0:
+            send(READY[j - 1], place <= h if h < max(PLACE) else None)
+
+    for n, names in ((1, [("x", 0), ("corner", 1)]), (0, [("x", 3)])):
+        @pl.when(sends_x)
+        def _():
+            pl.semaphore_wait(x_ready.at[n], 1)
+
+        send(names)
 
     for j, block in enumerate(blocks):
         @pl.when(both(gy == gz, gz == block))
@@ -426,11 +459,10 @@
         out_bound[:, b, :] = bound
         out_active[:, b, :] = active
 
-    for j in range(BLOCKS):
-        for _, when, copy in copies[j]:
-            @pl.when(when)
-            def _():
-                copy.wait_send()
+    for when, copy in copies.values():
+        @pl.when(when)
+        def _():
+            copy.wait_send()
 
 
 def write_out(bound, active, out_bound, out_active, sems):
@@ -492,6 +524,7 @@
             dma((4,)),
             dma((4,)),
             dma((4,)),
+            pltpu.SemaphoreType.REGULAR((2,)),
         ],
         compiler_params=pltpu.CompilerParams(
             collective_id=0, has_side_effects=True, vmem_limit_bytes=60 * 1024 * 1024

time: 13.2 us -> 12.8 us (0.970)
  the two profiles are of different devices: /device:TPU:97 before, /device:TPU:89 now
where the time goes in v4:
time: 12.8 us; the launch traced here: 12.7 us
  Pallas kernels  12.1 us (95%)
  between operations  0.64 us (5%)
    pallas_call x1, Pallas kernels, per_device(): pl.pallas_call(kernel, out_shape=(kept, kept), in_specs=[anywhere] * 12,...  11.5 us
    pallas_call x1, Pallas kernels, per_device(): pl.pallas_call(write_out, out_shape=(small, small), in_specs=[vmem, vmem]...  0.62 us

profile of v4, /device:TPU:89, one launch (start us, length us, event | category | flops | bytes accessed | tf_op | source)
XLA Modules:
  0.0 12.7 jit_solution(5859282396683435035)
XLA Ops:
  0.6 11.5 %restrict_and_step.1 = (f32[8,2,128]{2,1,0:T(2,128)S(1)}, f32[8,2,128]{2,1,0:T(2,128)S(1)}) custom-call(f32[8,32,32,128]{3,2,1,0:T(8,128)} %cal.1, f32[8,32,32,128]{3,2,1,0:T(8,128)} %act.1, s32[2,128]{1,0:T(2,128)} %bitcast.8, f32[2,128]{1,0:T(2,128)} %bitcast.9, s32[4,128]{1,0:T(4,128)} %bitcast.6, f32[4,128]{1,0:T(4,128)} %bitcast.7, s32[1,128]{1,0:T(1,128)} %bitcast.10, ...), custom_call_target="tpu_custom_call" | custom-call | tf_op jit(solution)/shard_map/restrict_and_step/pallas_call | solution.py:489
  12.1 0.6 %write_out.1 = (f32[8,2,128]{2,1,0:T(2,128)}, f32[8,2,128]{2,1,0:T(2,128)}) custom-call(f32[8,2,128]{2,1,0:T(2,128)S(1)} %get-tuple-element.4.bound, f32[8,2,128]{2,1,0:T(2,128)S(1)} %get-tuple-element.5.active), custom_call_target="tpu_custom_call" | custom-call | tf_op jit(solution)/shard_map/write_out/pallas_call | solution.py:540

commit v5 on v4

--- a/solution.py
+++ b/solution.py
@@ -20,9 +20,11 @@
 ROWS = 32
 CHUNKS = 4
 ORDER = (3, 0, 1, 2)
-PLACE = (4, 4, 4, 4, 4, 4)
-MAIN = CHUNKS * 16 + 16
-EDGE = CHUNKS * 8 + 8
+PLACE = (4, 4, 2, 2, 4, 4)
+MAIN = CHUNKS * 16 + 2
+EDGE = CHUNKS * 8 + 1
+CROSS = CHUNKS * 2 + 1
+CORNER = CHUNKS + 1
 
 
 def raw_weights(element, offset, node):
@@ -225,11 +227,11 @@
         turned_edge = jnp.transpose(jnp.broadcast_to(own[32:33], (128, 128)))
         for k in range(4):
             group = lax.rem(gy + k, 4)
-            edge_lane = 32 * lax.rem(gy + 1 + k, 4)
+            edge_group = lax.rem(gy + 1 + k, 4)
             wide = jnp.concatenate(
                 [
                     jnp.where(lane_w // 32 == group, turned, 0.0),
-                    jnp.where(lane_w == edge_lane, turned_edge, 0.0),
+                    jnp.where(lane_w // 32 == edge_group, turned_edge, 0.0),
                 ],
                 axis=1,
             )
@@ -238,8 +240,9 @@
             w2l[128 * k : 128 * (k + 1), :] = low
 
     def remote(src, dst, send_sem, recv_sem, x, y, z):
+        rows = {72: MAIN, 40: EDGE, 16: CROSS, 8: CORNER}[src.shape[0]]
         return pltpu.make_async_remote_copy(
-            src_ref=src, dst_ref=dst, send_sem=send_sem, recv_sem=recv_sem,
+            src_ref=src.at[pl.ds(0, rows)], dst_ref=dst.at[pl.ds(0, rows)], send_sem=send_sem, recv_sem=recv_sem,
             device_id={"gx": x, "gy": y, "gz": z}, device_id_type=MESH,
         )
 
@@ -261,43 +264,59 @@
                 y_buf[slot, ROWS * n : ROWS * (n + 1), columns] = high
                 y_buf[slot, ROWS * (2 + n) : ROWS * (3 + n), columns] = low
 
-    def finish(j, u, part):
+    sub_wide = iota((8, 256), 0)
+    within = lax.rem(iota((8, 128), 1), 32)
+
+    def chosen(where, value):
+        return jnp.where(where, value[:, 128:256], 0.0)
+
+    def finish(j, u, rows):
+        parts = [rows[8 * n : 8 * (n + 1)] for n in range(4)]
         if blocks[j] > 0 and j > 0:
             corner = pltpu.roll(tail[u, 8:16, :], 6, axis=0)
-            part = [
-                part[0:8] + tail[u, 0:8, :],
-                part[8:16],
-                part[16:24],
-                part[24:32] + jnp.where(sub8 == 0, corner, 0.0),
-            ]
-        else:
-            part = [part[8 * n : 8 * (n + 1)] for n in range(4)]
+            parts[0] += tail[u, 0:8, :]
+            parts[3] += jnp.where(sub_wide == 0, corner, 0.0)
         if j < BLOCKS - 1:
-            tail[u, 0:8, :] = part[2]
-            tail[u, 8:16, :] = part[3]
-        s_main[j, 16 * u : 16 * u + 8, :] = part[0]
-        s_main[j, 16 * u + 8 : 16 * u + 16, :] = part[1]
-        s_x[j, 2 * u : 2 * (u + 1), :] = part[3][0:2]
+            tail[u, 0:8, :] = parts[2]
+            tail[u, 8:16, :] = parts[3]
+        s_main[j, 16 * u : 16 * u + 8, :] = parts[0][:, 0:128]
+        s_main[j, 16 * u + 8 : 16 * u + 16, :] = parts[1][:, 0:128]
+        s_x[j, 2 * u : 2 * (u + 1), :] = parts[3][0:2, 0:128]
         if j in (0, BLOCKS - 1):
             slot = 0 if j == 0 else 1
-            s_edge[slot, 8 * u : 8 * (u + 1), :] = part[2]
-            s_corner[slot, u : u + 1, :] = part[3][2:3]
+            s_edge[slot, 8 * u : 8 * (u + 1), :] = parts[2][:, 0:128]
+            s_corner[slot, u : u + 1, :] = parts[3][2:3, 0:128]
+        first = 16 * (u % 2)
+        main = chosen(within == first + 15 - sub8, parts[0]) + chosen(within == first + 7 - sub8, parts[1])
+        cross = chosen(jnp.logical_and(sub8 < 2, within == 7 - 2 * u - sub8), parts[3])
+        edge = chosen(within == 8 * u + 7 - sub8, parts[2])
+        corner = chosen(jnp.logical_and(sub8 == 2, within == u), parts[3])
+        return main, cross, edge, corner
 
     def second_stage(j, f):
         y = y_buf[(2 * j + f) % 2]
         twice = dot(y, w2h[...])
         n = 2 * ROWS
         z = twice[0:n] + twice[n:] + dot(y[0:n], w2l[...])
-        extra = 0.0 if f == 0 else extra_buf[...]
-        for n in range(2):
-            u = 2 * f + n
-            rows = z[ROWS * n : ROWS * (n + 1)]
-            finish(j, u, rows[:, 0:128])
-            extra += pltpu.roll(rows[:, 128:256], u, axis=1) if u else rows[:, 128:256]
+        sums = [
+            a + b
+            for a, b in zip(finish(j, 2 * f, z[0:ROWS]), finish(j, 2 * f + 1, z[ROWS:]))
+        ]
+
+        def row_of(value):
+            return jnp.sum(value, axis=0, keepdims=True)
+
+        s_main[j, 16 * CHUNKS + f : 16 * CHUNKS + f + 1, :] = row_of(sums[0])
         if f == 0:
-            extra_buf[...] = extra
+            for n in range(3):
+                extra_buf[8 * n : 8 * (n + 1), :] = sums[n + 1]
         else:
-            finish(j, CHUNKS, extra)
+            rest = [row_of(sums[n + 1] + extra_buf[8 * n : 8 * (n + 1), :]) for n in range(3)]
+            s_x[j, CROSS - 1 : CROSS, :] = rest[0]
+            if j in (0, BLOCKS - 1):
+                slot = 0 if j == 0 else 1
+                s_edge[slot, EDGE - 1 : EDGE, :] = rest[1]
+                s_corner[slot, CORNER - 1 : CORNER, :] = rest[2]
 
     both = jnp.logical_and
     copies = {}
@@ -326,7 +345,7 @@
         [("x", 2), ("main", 2)],
         [("main", 3), ("edge", 1)],
     ]
-    RANK = {"x": 0, "corner": 1, "edge": 2, "main": 3}
+    RANK = {name: n for n, name in enumerate((("x", 1), ("corner", 0), ("main", 1), ("edge", 0), ("main", 0), ("x", 2), ("main", 2), ("main", 3), ("edge", 1)))}
 
     def send(names, when=None):
         for name in names:
@@ -370,10 +389,10 @@
         if h in PLACE:
             here = place == h
             enter(here)
-            names = [name for i in range(j - 1) for name in READY[i]]
-            send(sorted(names, key=lambda name: RANK[name[0]]), here)
-        if h >= min(PLACE) and f == 0:
-            send(READY[j - 1], place <= h if h < max(PLACE) else None)
+            names = [name for i in range(j) for name in READY[i]]
+            send(sorted(names, key=lambda name: RANK[name]), here)
+        if h > min(PLACE) and f == 0:
+            send(READY[j - 1], place < h)
 
     for n, names in ((1, [("x", 0), ("corner", 1)]), (0, [("x", 3)])):
         @pl.when(sends_x)
@@ -424,21 +443,41 @@
         )
         return low_rows, high_rows
 
+    def unpicked(row, shift):
+        return pltpu.roll(
+            jnp.broadcast_to(row, (8, 128)), shift % 128, axis=1, stride=1, stride_axis=0
+        )
+
+    crosses = [unpicked(r_x[c, CROSS - 1 : CROSS, :], 121) for c in range(4)]
+
+    def edges_of(c, u):
+        row = 16 * CHUNKS + u // 2
+        row = r_main[c, row : row + 1, :]
+        corner = r_corner[c, CORNER - 1 : CORNER, :]
+        corner = pltpu.roll(corner, 128 - u, axis=1) if u else corner
+        cross = crosses[c]
+        low_rows = (
+            unpicked(row, 113 - 16 * (u % 2))
+            + unpicked(r_edge[c, EDGE - 1 : EDGE, :], 121 - 8 * u)
+            + jnp.where(top, cross[2 * u : 2 * u + 1] + corner, 0.0)
+        )
+        high_rows = unpicked(row, 121 - 16 * (u % 2)) + jnp.where(
+            top, cross[2 * u + 1 : 2 * u + 2], 0.0
+        )
+        return low_rows, high_rows
+
     def by_group(values, shift):
         out = values[(0 - shift) % 4]
         for h in range(1, 4):
             out = jnp.where(group == h, values[(h - shift) % 4], out)
         return out
 
-    extras = [gathered(c, CHUNKS) for c in range(4)]
     drive = {}
     for u in range(CHUNKS):
         mains = [gathered(c, u) for c in range(4)]
+        picked = [edges_of(c, u) for c in range(4)]
         for b in range(2):
-            edges = [
-                pltpu.roll(extras[c][b], 128 - u, axis=1) if u else extras[c][b] for c in range(4)
-            ]
-            edges = [jnp.where(lead, value, 0.0) for value in edges]
+            edges = [jnp.where(lead, picked[c][b], 0.0) for c in range(4)]
             for k in range(4):
                 value = by_group([mains[c][b] for c in range(4)], k) + by_group(edges, k + 1)
                 if k:
@@ -504,15 +543,15 @@
             pltpu.VMEM((512, 256), bf16),
             pltpu.VMEM((512, 256), bf16),
             pltpu.VMEM((2, 4 * ROWS, 512), bf16),
-            pltpu.VMEM((CHUNKS + 1, 16, 128), f32),
-            pltpu.VMEM((ROWS, 128), f32),
-            pltpu.VMEM((BLOCKS, MAIN, 128), f32),
+            pltpu.VMEM((CHUNKS, 16, 256), f32),
+            pltpu.VMEM((24, 128), f32),
+            pltpu.VMEM((BLOCKS, 72, 128), f32),
             pltpu.VMEM((BLOCKS, 16, 128), f32),
-            pltpu.VMEM((2, EDGE, 128), f32),
+            pltpu.VMEM((2, 40, 128), f32),
             pltpu.VMEM((2, 8, 128), f32),
-            pltpu.VMEM((4, MAIN, 128), f32),
+            pltpu.VMEM((4, 72, 128), f32),
             pltpu.VMEM((4, 16, 128), f32),
-            pltpu.VMEM((4, EDGE, 128), f32),
+            pltpu.VMEM((4, 40, 128), f32),
             pltpu.VMEM((4, 8, 128), f32),
             dma((BLOCKS, CHUNKS)),
             dma((10,)),

time: 12.8 us -> 12.8 us (level)
  no operation moved by 1% of the time
where the time goes in v5:
time: 12.8 us; the launch traced here: 12.6 us
  Pallas kernels  12 us (94%)
  between operations  0.64 us (5%)
    pallas_call x1, Pallas kernels, per_device(): pl.pallas_call(kernel, out_shape=(kept, kept), in_specs=[anywhere] * 12,...  11.3 us
    pallas_call x1, Pallas kernels, per_device(): pl.pallas_call(write_out, out_shape=(small, small), in_specs=[vmem, vmem]...  0.62 us

profile of v5, /device:TPU:89, one launch (start us, length us, event | category | flops | bytes accessed | tf_op | source)
XLA Modules:
  0.0 12.6 jit_solution(12045519302188524885)
XLA Ops:
  0.6 11.3 %restrict_and_step.1 = (f32[8,2,128]{2,1,0:T(2,128)S(1)}, f32[8,2,128]{2,1,0:T(2,128)S(1)}) custom-call(f32[8,32,32,128]{3,2,1,0:T(8,128)} %cal.1, f32[8,32,32,128]{3,2,1,0:T(8,128)} %act.1, s32[2,128]{1,0:T(2,128)} %bitcast.8, f32[2,128]{1,0:T(2,128)} %bitcast.9, s32[4,128]{1,0:T(4,128)} %bitcast.6, f32[4,128]{1,0:T(4,128)} %bitcast.7, s32[1,128]{1,0:T(1,128)} %bitcast.10, ...), custom_call_target="tpu_custom_call" | custom-call | tf_op jit(solution)/shard_map/restrict_and_step/pallas_call | solution.py:528
  12.0 0.6 %write_out.1 = (f32[8,2,128]{2,1,0:T(2,128)}, f32[8,2,128]{2,1,0:T(2,128)}) custom-call(f32[8,2,128]{2,1,0:T(2,128)S(1)} %get-tuple-element.4.bound, f32[8,2,128]{2,1,0:T(2,128)S(1)} %get-tuple-element.5.active), custom_call_target="tpu_custom_call" | custom-call | tf_op jit(solution)/shard_map/write_out/pallas_call | solution.py:579

commit v6 on v5

--- a/solution.py
+++ b/solution.py
@@ -19,8 +19,8 @@
 BLOCKS = 4
 ROWS = 32
 CHUNKS = 4
-ORDER = (3, 0, 1, 2)
-PLACE = (4, 4, 2, 2, 4, 4)
+ORDER = (0, 3, 1, 2)
+PLACE = (4, 4, 2, 2, 4, 4, 3, 3)
 MAIN = CHUNKS * 16 + 2
 EDGE = CHUNKS * 8 + 1
 CROSS = CHUNKS * 2 + 1
@@ -272,18 +272,18 @@
 
     def finish(j, u, rows):
         parts = [rows[8 * n : 8 * (n + 1)] for n in range(4)]
-        if blocks[j] > 0 and j > 0:
+        if blocks[j] in (1, 2):
             corner = pltpu.roll(tail[u, 8:16, :], 6, axis=0)
             parts[0] += tail[u, 0:8, :]
             parts[3] += jnp.where(sub_wide == 0, corner, 0.0)
-        if j < BLOCKS - 1:
+        if blocks[j] in (0, 1):
             tail[u, 0:8, :] = parts[2]
             tail[u, 8:16, :] = parts[3]
         s_main[j, 16 * u : 16 * u + 8, :] = parts[0][:, 0:128]
         s_main[j, 16 * u + 8 : 16 * u + 16, :] = parts[1][:, 0:128]
         s_x[j, 2 * u : 2 * (u + 1), :] = parts[3][0:2, 0:128]
-        if j in (0, BLOCKS - 1):
-            slot = 0 if j == 0 else 1
+        if blocks[j] in (2, 3):
+            slot = 3 - blocks[j]
             s_edge[slot, 8 * u : 8 * (u + 1), :] = parts[2][:, 0:128]
             s_corner[slot, u : u + 1, :] = parts[3][2:3, 0:128]
         first = 16 * (u % 2)
@@ -313,8 +313,8 @@
         else:
             rest = [row_of(sums[n + 1] + extra_buf[8 * n : 8 * (n + 1), :]) for n in range(3)]
             s_x[j, CROSS - 1 : CROSS, :] = rest[0]
-            if j in (0, BLOCKS - 1):
-                slot = 0 if j == 0 else 1
+            if blocks[j] in (2, 3):
+                slot = 3 - blocks[j]
                 s_edge[slot, EDGE - 1 : EDGE, :] = rest[1]
                 s_corner[slot, CORNER - 1 : CORNER, :] = rest[2]
 
@@ -323,7 +323,7 @@
     for j, block in enumerate(blocks):
         copies["x", j] = (sends_x, remote(
             s_x.at[j], r_x.at[gy], ss_x.at[j], rs_x.at[gy], gx + 1, gz, block))
-        if j == 0:
+        if block == BLOCKS - 1:
             copies["corner", 0] = (both(sends_edge, sends_x), remote(
                 s_corner.at[0], r_corner.at[gy], ss_corner.at[0], rs_corner.at[gy],
                 gx + 1, gz + 1, 0))
@@ -340,12 +340,14 @@
                 gx, gz, BLOCKS - 1))
 
     READY = [
-        [("corner", 0), ("edge", 0), ("main", 0)],
-        [("x", 1), ("main", 1)],
+        [("x", 0), ("main", 0)],
+        [("corner", 0), ("edge", 0), ("main", 1)],
         [("x", 2), ("main", 2)],
         [("main", 3), ("edge", 1)],
     ]
-    RANK = {name: n for n, name in enumerate((("x", 1), ("corner", 0), ("main", 1), ("edge", 0), ("main", 0), ("x", 2), ("main", 2), ("main", 3), ("edge", 1)))}
+    RANK = {name: n for n, name in enumerate((
+        ("x", 0), ("corner", 0), ("main", 0), ("edge", 0), ("main", 1),
+        ("x", 2), ("main", 2), ("main", 3), ("edge", 1)))}
 
     def send(names, when=None):
         for name in names:
@@ -373,8 +375,13 @@
         def _():
             pl.semaphore_signal(x_ready.at[lax.max(gz - 2, 0)], inc=1)
 
-    place = jnp.where(gx == 3, jnp.where(gz == 2, PLACE[5], PLACE[4]), jnp.where(
-        gz == 0, PLACE[0], jnp.where(gz == 1, PLACE[1], jnp.where(gz == 2, PLACE[2], PLACE[3]))))
+    def by_gz(values):
+        out = values[3]
+        for n in range(3):
+            out = jnp.where(gz == n, values[n], out)
+        return out
+
+    place = jnp.where(gx == 3, by_gz(PLACE[4:]), by_gz(PLACE[:4]))
     for h in range(2 * BLOCKS + 1):
         j, f = h // 2, h % 2
         if h < 2 * BLOCKS:
@@ -394,7 +401,7 @@
         if h > min(PLACE) and f == 0:
             send(READY[j - 1], place < h)
 
-    for n, names in ((1, [("x", 0), ("corner", 1)]), (0, [("x", 3)])):
+    for n, names in ((1, [("x", 1), ("corner", 1)]), (0, [("x", 3)])):
         @pl.when(sends_x)
         def _():
             pl.semaphore_wait(x_ready.at[n], 1)

time: 12.8 us -> 12.7 us (level)
  no operation moved by 1% of the time
where the time goes in v6:
time: 12.7 us; the launch traced here: 12.6 us
  Pallas kernels  12 us (94%)
  between operations  0.64 us (5%)
    pallas_call x1, Pallas kernels, per_device(): pl.pallas_call(kernel, out_shape=(kept, kept), in_specs=[anywhere] * 12,...  11.3 us
    pallas_call x1, Pallas kernels, per_device(): pl.pallas_call(write_out, out_shape=(small, small), in_specs=[vmem, vmem]...  0.62 us

profile of v6, /device:TPU:89, one launch (start us, length us, event | category | flops | bytes accessed | tf_op | source)
XLA Modules:
  0.0 12.6 jit_solution(10272690094924528593)
XLA Ops:
  0.6 11.3 %restrict_and_step.1 = (f32[8,2,128]{2,1,0:T(2,128)S(1)}, f32[8,2,128]{2,1,0:T(2,128)S(1)}) custom-call(f32[8,32,32,128]{3,2,1,0:T(8,128)} %cal.1, f32[8,32,32,128]{3,2,1,0:T(8,128)} %act.1, s32[2,128]{1,0:T(2,128)} %bitcast.8, f32[2,128]{1,0:T(2,128)} %bitcast.9, s32[4,128]{1,0:T(4,128)} %bitcast.6, f32[4,128]{1,0:T(4,128)} %bitcast.7, s32[1,128]{1,0:T(1,128)} %bitcast.10, ...), custom_call_target="tpu_custom_call" | custom-call | tf_op jit(solution)/shard_map/restrict_and_step/pallas_call | solution.py:535
  12.0 0.6 %write_out.1 = (f32[8,2,128]{2,1,0:T(2,128)}, f32[8,2,128]{2,1,0:T(2,128)}) custom-call(f32[8,2,128]{2,1,0:T(2,128)S(1)} %get-tuple-element.4.bound, f32[8,2,128]{2,1,0:T(2,128)S(1)} %get-tuple-element.5.active), custom_call_target="tpu_custom_call" | custom-call | tf_op jit(solution)/shard_map/write_out/pallas_call | solution.py:586

commit v7 on v6

--- a/solution.py
+++ b/solution.py
@@ -426,13 +426,24 @@
         def _():
             remote(source, buf.at[c], ss_main.at[0], sems.at[c], gx, gy, gz).wait_recv()
 
+    for n in range(6, 10):
+        smalls[n].wait()
+    for when, copy in copies.values():
+        @pl.when(when)
+        def _():
+            copy.wait_send()
+
     for c in range(4):
         arrive(jnp.logical_not(main_self(c)), r_main, rs_main, c, s_main.at[0])
-        arrive(jnp.logical_and(has_edge, jnp.logical_not(jnp.logical_or(below_self(c), both(last_self, gy == c)))), r_edge, rs_edge, c, s_edge.at[0])
+    for c in range(4):
+        arrive(
+            both(has_edge, jnp.logical_not(jnp.logical_or(below_self(c), both(last_self, gy == c)))),
+            r_edge, rs_edge, c, s_edge.at[0],
+        )
+    for c in range(4):
+        arrive(both(has_x, has_edge), r_corner, rs_corner, c, s_corner.at[0])
+    for c in range(4):
         arrive(has_x, r_x, rs_x, c, s_x.at[0])
-        arrive(jnp.logical_and(has_x, has_edge), r_corner, rs_corner, c, s_corner.at[0])
-    for n in range(6, 10):
-        smalls[n].wait()
 
     top = sub8 == 0
     lane = iota((8, 128), 1)
@@ -504,11 +515,6 @@
             active = active * keep_active + pull * bound
         out_bound[:, b, :] = bound
         out_active[:, b, :] = active
-
-    for when, copy in copies.values():
-        @pl.when(when)
-        def _():
-            copy.wait_send()
 
 
 def write_out(bound, active, out_bound, out_active, sems):

time: 12.7 us -> 12.7 us (level)
  no operation moved by 1% of the time
where the time goes in v7:
time: 12.7 us; the launch traced here: 12.6 us
  Pallas kernels  11.9 us (94%)
  between operations  0.64 us (5%)
    pallas_call x1, Pallas kernels, per_device(): pl.pallas_call(kernel, out_shape=(kept, kept), in_specs=[anywhere] * 12,...  11.3 us
    pallas_call x1, Pallas kernels, per_device(): pl.pallas_call(write_out, out_shape=(small, small), in_specs=[vmem, vmem]...  0.62 us

profile of v7, /device:TPU:89, one launch (start us, length us, event | category | flops | bytes accessed | tf_op | source)
XLA Modules:
  0.0 12.6 jit_solution(16057011984627344902)
XLA Ops:
  0.6 11.3 %restrict_and_step.1 = (f32[8,2,128]{2,1,0:T(2,128)S(1)}, f32[8,2,128]{2,1,0:T(2,128)S(1)}) custom-call(f32[8,32,32,128]{3,2,1,0:T(8,128)} %cal.1, f32[8,32,32,128]{3,2,1,0:T(8,128)} %act.1, s32[2,128]{1,0:T(2,128)} %bitcast.8, f32[2,128]{1,0:T(2,128)} %bitcast.9, s32[4,128]{1,0:T(4,128)} %bitcast.6, f32[4,128]{1,0:T(4,128)} %bitcast.7, s32[1,128]{1,0:T(1,128)} %bitcast.10, ...), custom_call_target="tpu_custom_call" | custom-call | tf_op jit(solution)/shard_map/restrict_and_step/pallas_call | solution.py:541
  11.9 0.6 %write_out.1 = (f32[8,2,128]{2,1,0:T(2,128)}, f32[8,2,128]{2,1,0:T(2,128)}) custom-call(f32[8,2,128]{2,1,0:T(2,128)S(1)} %get-tuple-element.4.bound, f32[8,2,128]{2,1,0:T(2,128)S(1)} %get-tuple-element.5.active), custom_call_target="tpu_custom_call" | custom-call | tf_op jit(solution)/shard_map/write_out/pallas_call | solution.py:592
